TPU v7x, 512 devices: a whole 4x4x16 slice. The times are simulated.
512 devices in a mesh: orb: 32 (over z, core), grp: 16 (over y, x).
Axes of the slice: x: 4, y: 4, z: 16, core: 2. Of those that a mesh axis runs over, the one named last changes fastest.
Arguments:
- orbitals: bfloat16 [2048, 32, 1024], P('orb', 'grp'), may hold values from -6 to 6
- pair_list: int32 [32, 32, 3], replicated, may hold values from 0 to 63, as said below
- offsets: int32 [2048, 3], replicated, may hold values from 0 to 15
Outputs:
- exchange_action: float32 [2048, 32, 1024], P('orb', 'grp')
Inputs may be any that keep to these rules, and one draw needn't show every extreme that they name: pair_list[o, r, 0] and pair_list[o, r, 1] are below 64; pair_list[o, r, 2] is a slot below 64, distinct within each block o, so a block names each owner group at most 2 times; in every draw some owner group is named 2 times by every block; the two orbitals of a pair differ.
All inputs are finite; a program needn't handle non-finite values.
Results may differ from a plain program's by a relative error of at most 0.0006.
Values may be sent and summed in bfloat16 or wider, within the bound.
No kernel may reach another device: no remote copies, remote signals or barrier semaphores. Data moves between devices by JAX's collectives and lax.ppermute only.
A program may use at most 64 MiB of HBM per device.

v0:
```python
import functools
import math

import jax
import jax.numpy as jnp
from jax import lax
from jax.experimental import pallas as pl
from jax.experimental.pallas import tpu as pltpu
from jax.sharding import PartitionSpec as P

BOX = 32
PLANE = BOX * BOX
ORB_GRP = 64
CAP = 2
SCREEN = 0.25
LANES = 128
TOP_EXP = 14.0
highest = lax.Precision.HIGHEST


def sine_table():
    counts = jnp.arange(BOX).astype(jnp.float32) + 1.0
    return jnp.sqrt(2.0 / (BOX + 1.0)) * jnp.sin(
        math.pi * counts[:, None] * counts[None, :] / (BOX + 1.0)
    )


def green_rows():
    levels = 2.0 - 2.0 * jnp.cos(
        math.pi * (jnp.arange(BOX).astype(jnp.float32) + 1.0) / (BOX + 1.0)
    )
    lanes = jnp.arange(PLANE, dtype=jnp.int32)

    def level(index):
        return 2.0 - 2.0 * jnp.cos(math.pi * (index.astype(jnp.float32) + 1.0) / (BOX + 1.0))

    return 1.0 / (levels[:, None] + (level(lanes // BOX) + level(lanes % BOX))[None, :] + SCREEN)


def halves(value):
    high = value.astype(jnp.bfloat16)
    return high, (value - high.astype(jnp.float32)).astype(jnp.bfloat16)


def dot(a, b):
    return jnp.dot(a, b, preferred_element_type=jnp.float32)


def plane_kernel(sine_ref, high_ref, low_ref):
    lane = lax.broadcasted_iota(jnp.int32, (BOX, PLANE), 1)
    row = lax.broadcasted_iota(jnp.int32, (BOX, PLANE), 0)
    by_y = jnp.where((lane >> 5) == row, 1.0, 0.0).astype(jnp.bfloat16)
    by_z = jnp.where((lane & (BOX - 1)) == row, 1.0, 0.0).astype(jnp.bfloat16)
    sine = sine_ref[...]
    parts = []
    rest = sine
    for _ in range(3):
        piece = rest.astype(jnp.bfloat16)
        parts.append(piece)
        rest = rest - piece.astype(jnp.float32)
    cols_y = dot(parts[0], by_y) + dot(parts[1], by_y) + dot(parts[2], by_y)
    cols_z = dot(parts[0], by_z) + dot(parts[1], by_z) + dot(parts[2], by_z)
    for m in range(BOX):
        block = cols_y[m : m + 1, :] * cols_z
        high = block.astype(jnp.bfloat16)
        high_ref[pl.ds(m * BOX, BOX), :] = high
        low_ref[pl.ds(m * BOX, BOX), :] = (block - high.astype(jnp.float32)).astype(jnp.bfloat16)


def plane_tables(sine):
    shape = jax.ShapeDtypeStruct((PLANE, PLANE), jnp.bfloat16)
    return pl.pallas_call(plane_kernel, out_shape=(shape, shape), name="plane_tables")(sine)


def pair_kernel(
    share, moves_ref, boxes_ref, high_ref, low_ref, green_ref, sine_ref, out_ref, first, second
):
    depth = boxes_ref.shape[1]
    sides = BOX // depth
    rows = share * BOX
    for s in range(sides):
        for k in range(share):
            piece = boxes_ref[s * share + k].astype(jnp.float32)
            at = k * BOX + s * depth
            first[at : at + depth, :] = piece[:, :PLANE]
            second[at : at + depth, :] = piece[:, PLANE:]

    row = lax.broadcasted_iota(jnp.int32, (rows, rows), 0)
    col = lax.broadcasted_iota(jnp.int32, (rows, rows), 1)
    same = (row >> 5) == (col >> 5)
    step = jnp.zeros((rows, rows), jnp.int32)
    for k in range(share):
        step = jnp.where((row >> 5) == k, moves_ref[k, 0], step)
    ahead = jnp.where(same & (col == row + step), 1.0, 0.0).astype(jnp.bfloat16)
    back = jnp.where(same & (row == col + step), 1.0, 0.0).astype(jnp.bfloat16)

    lane = lax.broadcasted_iota(jnp.int32, (BOX, PLANE), 1)
    y, z = lane >> 5, lane & (BOX - 1)

    def moved(value, dy, dz):
        turned = pltpu.roll(value, (PLANE - (dy * BOX + dz)) & (PLANE - 1), 1)
        inside = (y + dy >= 0) & (y + dy < BOX) & (z + dz >= 0) & (z + dz < BOX)
        return jnp.where(inside, turned, 0.0)

    sine = sine_ref[...]
    wide = jnp.concatenate([jnp.concatenate([sine] * share, 1)] * share, 0)
    wide = jnp.where(same, wide, 0.0)
    sine_high, sine_low = halves(wide)
    sine_three = jnp.concatenate([sine_high, sine_high, sine_low], 1)

    def along_x(value):
        high, low = halves(value)
        return dot(sine_three, jnp.concatenate([high, low, high], 0))

    def along_plane(value):
        high, low = halves(value)
        both = dot(jnp.concatenate([high, low], 0), high_ref[...])
        return both[:rows] + both[rows:] + dot(high, low_ref[...])

    turned = [
        moved(second[k * BOX : (k + 1) * BOX, :], moves_ref[k, 1], moves_ref[k, 2])
        for k in range(share)
    ]
    shifted = dot(ahead, jnp.concatenate(turned, 0).astype(jnp.bfloat16))
    own = first[...]
    modes = along_plane(along_x(own * shifted))
    modes = modes * jnp.concatenate([green_ref[...]] * share, 0)
    potential = along_x(along_plane(modes))

    to_first = potential * shifted
    high, low = halves(potential * own)
    upright = dot(jnp.concatenate([back, back], 1), jnp.concatenate([high, low], 0))
    for k in range(share):
        part = slice(k * BOX, (k + 1) * BOX)
        returned = moved(upright[part], -moves_ref[k, 1], -moves_ref[k, 2])
        mine = to_first[part]
        peak = jnp.max(
            jnp.maximum(jnp.abs(mine), jnp.abs(returned)), axis=(0, 1), keepdims=True
        )
        power = jnp.floor(TOP_EXP - jnp.log2(jnp.maximum(peak, 1e-30)))
        gain = jnp.exp2(power)
        first[part, :] = mine * gain
        second[part, :] = returned * gain
        note = jnp.broadcast_to(power, (depth, LANES))
        for s in range(sides):
            at = k * BOX + s * depth
            out_ref[s * share + k, :, 0:PLANE] = first[at : at + depth, :]
            out_ref[s * share + k, :, PLANE : PLANE + LANES] = note
            out_ref[s * share + k, :, PLANE + LANES :] = second[at : at + depth, :]


def pair_terms(boxes, moves, high, low, green, sine):
    rows, depth, _ = boxes.shape
    share = moves.shape[0]
    vmem = pl.BlockSpec(memory_space=pltpu.VMEM)
    return pl.pallas_call(
        functools.partial(pair_kernel, share),
        out_shape=jax.ShapeDtypeStruct((rows, depth, 2 * PLANE + LANES), jnp.float32),
        in_specs=[pl.BlockSpec(memory_space=pltpu.SMEM)] + [vmem] * 5,
        out_specs=vmem,
        scratch_shapes=[pltpu.VMEM((share * BOX, PLANE), jnp.float32)] * 2,
        name="pair_terms",
    )(moves, boxes, high, low, green, sine)


def per_device(orbitals, pair_list, offsets):
    groups = lax.axis_size("orb")
    layers = lax.axis_size("grp")
    me = lax.axis_index("orb")
    region = lax.axis_index("grp")
    held, depth, plane = orbitals.shape
    slot_count = groups * CAP
    pair_count = pair_list.shape[1]
    share = pair_count // layers

    wanted = me * CAP + jnp.arange(CAP, dtype=jnp.int32)
    asked = pair_list[:, None, :, 2] == wanted[None, :, None]
    asked_valid = jnp.any(asked, axis=2).reshape(slot_count)
    asked_local = jnp.sum(jnp.where(asked, pair_list[:, None, :, 1], 0), axis=2)
    asked_local = asked_local.reshape(slot_count)
    incoming = lax.all_to_all(
        jnp.take(orbitals, asked_local, axis=0), "orb", split_axis=0, concat_axis=0, tiled=True
    )

    own = lax.dynamic_index_in_dim(pair_list, me, 0, keepdims=False)
    first_local, second_local, slot = own[:, 0], own[:, 1], own[:, 2]
    rows = jnp.concatenate(
        [jnp.take(incoming, slot, axis=0), jnp.take(orbitals, first_local, axis=0)], axis=2
    )
    boxes = lax.all_to_all(rows, "grp", split_axis=0, concat_axis=0, tiled=True)

    part = lax.dynamic_slice_in_dim(own, region * share, share, 0)
    first_ids = me * ORB_GRP + part[:, 0]
    second_ids = part[:, 2] // CAP * ORB_GRP + part[:, 1]
    moves = jnp.take(offsets, first_ids, axis=0) - jnp.take(offsets, second_ids, axis=0)

    sine = sine_table()
    high, low = plane_tables(sine)
    terms = pair_terms(boxes, moves, high, low, green_rows(), sine).astype(jnp.float16)
    terms = lax.all_to_all(terms, "grp", split_axis=0, concat_axis=0, tiled=True)

    slot_hot = slot[None, :] == jnp.arange(slot_count, dtype=jnp.int32)[:, None]
    row_of_slot = jnp.sum(
        jnp.where(slot_hot, jnp.arange(pair_count, dtype=jnp.int32)[None, :], 0), axis=1
    )
    to_first = lax.all_to_all(
        jnp.take(terms[:, :, : plane + LANES], row_of_slot, axis=0),
        "orb",
        split_axis=0,
        concat_axis=0,
        tiled=True,
    )

    local_ids = jnp.arange(held, dtype=jnp.int32)[:, None]
    kept_gain = jnp.exp2(-terms[:, 0, plane].astype(jnp.float32))
    kept_hot = jnp.where(first_local[None, :] == local_ids, kept_gain[None, :], 0.0)
    back_gain = jnp.exp2(-to_first[:, 0, plane].astype(jnp.float32))
    back_hot = jnp.where(
        (asked_local[None, :] == local_ids) & asked_valid[None, :], back_gain[None, :], 0.0
    )
    kept = terms[:, :, plane + LANES :].astype(jnp.float32).reshape(pair_count, depth * plane)
    back = to_first[:, :, :plane].astype(jnp.float32).reshape(slot_count, depth * plane)
    action = jnp.dot(kept_hot, kept, precision=highest)
    action = action + jnp.dot(back_hot, back, precision=highest)
    return action.reshape(orbitals.shape)


def solution(mesh):
    return jax.shard_map(
        per_device,
        mesh=mesh,
        in_specs=(P("orb", "grp", None), P(), P()),
        out_specs=P("orb", "grp", None),
        check_vma=False,
    )
```

profile of v0, /device:TPU:1, one launch (start us, length us, event | category | flops | bytes accessed | tf_op | source)
XLA Modules:
  0.0 113.3 jit_solution(16037409307497739078)
XLA Ops:
  0.0 0.0 copy-start
  0.0 0.0 copy-start.2
  0.0 0.8 slice_bitcast_fusion.1
  0.8 0.2 fusion
  1.0 0.1 copy.19
  1.1 0.1 reshape.166
  1.2 0.1 reshape.167
  1.3 0.0 copy-done
  1.3 1.1 gather_fusion
  2.4 1.0 broadcast_select_fusion.1
  3.5 16.7 %all-to-all-start = ((bf16[64,2,1024]{2,1,0:T(2,128)(2,1)}), bf16[64,2,1024]{2,1,0:T(2,128)(2,1)S(1)}, u32[]{:S(2)}, u32[]{:S(2)}) async-start(bf16[64,2,1024]{2,1,0:T(2,128)(2,1)} %broadcast_select_fusion.1), calls=%async_computation | async-start | bytes 524288 | tf_op jit(solution)/shard_map/all_to_all | solution.py:181
  20.2 0.8 constant_dynamic-slice_fusion
  21.0 0.1 copy.16
  21.1 0.2 add_reduce_fusion
  21.3 0.7 constant_dynamic-slice_fusion.1
  22.1 0.1 fusion.33
  22.1 0.1 select_reduce_fusion
  22.3 0.8 gather_fusion.5
  23.1 0.0 copy-done.2
  23.1 0.4 copy.17
  23.5 0.6 gather_fusion.3
  24.0 0.6 gather_fusion.2
  24.6 0.6 select_subtract_fusion.moves_ref
  25.3 0.7 sine_multiply_fusion.sine_ref
  26.0 0.2 broadcast_select_fusion.2
  26.2 16.3 %all-to-all-done = bf16[64,2,1024]{2,1,0:T(2,128)(2,1)S(1)} async-done(((bf16[64,2,1024]{2,1,0:T(2,128)(2,1)}), bf16[64,2,1024]{2,1,0:T(2,128)(2,1)S(1)}, u32[]{:S(2)}, u32[]{:S(2)}) %all-to-all-start) | async-done | bytes 262176 | tf_op jit(solution)/shard_map/all_to_all | solution.py:181
  42.5 0.8 gather_fusion.4
  43.3 0.2 broadcast_select_fusion.3
  43.5 0.9 pad_maximum_fusion
  44.4 6.8 %all-to-all-start.1 = ((bf16[32,2,2048]{2,1,0:T(2,128)(2,1)}), bf16[32,2,2048]{2,1,0:T(2,128)(2,1)S(1)}, u32[]{:S(2)}, u32[]{:S(2)}) async-start(bf16[32,2,2048]{2,1,0:T(2,128)(2,1)} %pad_maximum_fusion), calls=%async_computation.1 | async-start | bytes 524288 | tf_op jit(solution)/shard_map/all_to_all | solution.py:190
  51.2 3.8 %plane_tables.1 = (bf16[1024,1024]{1,0:T(8,128)(2,1)}, bf16[1024,1024]{1,0:T(8,128)(2,1)}) custom-call(f32[32,32]{1,0:T(8,128)} %sine_multiply_fusion.sine_ref), custom_call_target="tpu_custom_call" | custom-call | tf_op jit(solution)/shard_map/plane_tables/pallas_call | solution.py:72
  55.0 0.7 add_divide_fusion.green_ref
  55.8 3.0 %all-to-all-done.1.boxes_ref = bf16[32,2,2048]{2,1,0:T(2,128)(2,1)S(1)} async-done(((bf16[32,2,2048]{2,1,0:T(2,128)(2,1)}), bf16[32,2,2048]{2,1,0:T(2,128)(2,1)S(1)}, u32[]{:S(2)}, u32[]{:S(2)}) %all-to-all-start.1) | async-done | bytes 262176 | tf_op jit(solution)/shard_map/all_to_all | solution.py:190
  58.8 0.0 copy-start.1
  58.8 0.7 copy-done.1
  59.5 5.8 %pair_terms.1 = f32[32,2,2176]{2,1,0:T(2,128)} custom-call(s32[2,3]{1,0:T(2,128)} %select_subtract_fusion.moves_ref, bf16[32,2,2048]{2,1,0:T(2,128)(2,1)} %copy-done.1, bf16[1024,1024]{1,0:T(8,128)(2,1)} %get-tuple-element.9.high_ref, bf16[1024,1024]{1,0:T(8,128)(2,1)} %get-tuple-element.10.low_ref, f32[32,1024]{1,0:T(8,128)} %add_divide_fusion.green_ref, ...), custom_call_target="tpu_custom_call" | custom-call | tf_op jit(solution)/shard_map/pair_terms/pallas_call | solution.py:156
  65.2 2.0 %convert_element_type.57 = f16[32,2,2176]{2,1,0:T(2,128)(2,1)} convert(f32[32,2,2176]{2,1,0:T(2,128)} %pair_terms.1) | non-fusion elementwise | flops 139264 | bytes 835584 | tf_op jit(solution)/shard_map/convert_element_type | solution.py:199
  67.2 3.7 %all-to-all-start.2 = ((f16[32,2,2176]{2,1,0:T(2,128)(2,1)}), f16[32,2,2176]{2,1,0:T(2,128)(2,1)S(1)}, u32[]{:S(2)}, u32[]{:S(2)}) async-start(f16[32,2,2176]{2,1,0:T(2,128)(2,1)} %convert_element_type.57), calls=%async_computation.2 | async-start | bytes 557056 | tf_op jit(solution)/shard_map/all_to_all | solution.py:200
  70.9 7.7 %all-to-all-done.2 = f16[32,2,2176]{2,1,0:T(2,128)(2,1)S(1)} async-done(((f16[32,2,2176]{2,1,0:T(2,128)(2,1)}), f16[32,2,2176]{2,1,0:T(2,128)(2,1)S(1)}, u32[]{:S(2)}, u32[]{:S(2)}) %all-to-all-start.2) | async-done | bytes 278560 | tf_op jit(solution)/shard_map/all_to_all | solution.py:200
  78.6 0.1 slice.62
  78.7 1.2 %gather_fusion.1 = f16[64,2,1152]{2,1,0:T(2,128)(2,1)S(1)} fusion(f16[32,2,1152]{2,1,0:T(2,128)(2,1)S(1)} %slice.62, s32[1024]{0:T(1024)S(1)} %pad_clamp_fusion), kind=kCustom, calls=%fused_computation.5 | custom fusion | bytes 590080 | tf_op jit(solution)/shard_map/jit(_take)/gather | solution.py:207
  79.9 1.1 broadcast_select_fusion
  81.0 6.5 %all-to-all-start.3 = ((f16[64,2,1152]{2,1,0:T(2,128)(2,1)}), f16[64,2,1152]{2,1,0:T(2,128)(2,1)S(1)}, u32[]{:S(2)}, u32[]{:S(2)}) async-start(f16[64,2,1152]{2,1,0:T(2,128)(2,1)} %broadcast_select_fusion), calls=%async_computation.3 | async-start | bytes 589824 | tf_op jit(solution)/shard_map/all_to_all | solution.py:206
  87.5 0.2 compare_reduce_fusion
  87.7 0.1 copy.21
  87.8 0.1 and.68
  87.9 0.1 slice.61
  88.1 0.3 fusion.19
  88.4 0.5 fusion.5
  88.9 21.8 %all-to-all-done.3 = f16[64,2,1152]{2,1,0:T(2,128)(2,1)S(1)} async-done(((f16[64,2,1152]{2,1,0:T(2,128)(2,1)}), f16[64,2,1152]{2,1,0:T(2,128)(2,1)S(1)}, u32[]{:S(2)}, u32[]{:S(2)}) %all-to-all-start.3) | async-done | bytes 294944 | tf_op jit(solution)/shard_map/all_to_all | solution.py:206
  110.7 0.2 slice.64
  110.9 0.1 copy.24
  111.0 0.6 fusion.7
  111.6 0.5 convolution_add_fusion
  112.1 1.2 %reshape.170 = f32[64,2,1024]{2,1,0:T(2,128)} reshape(f32[64,2048]{1,0:T(8,128)S(1)} %convolution_add_fusion) | data formatting | bytes 1048576 | tf_op jit(solution)/shard_map/reshape | solution.py:225
  (20 shorter events, 0.2 us)
Async XLA Ops:
  0.0 1.3 %copy-start = (bf16[64,2,1024]{2,1,0:T(2,128)(2,1)S(1)}, bf16[64,2,1024]{2,1,0:T(2,128)(2,1)}, u32[]{:S(2)}) copy-start(bf16[64,2,1024]{2,1,0:T(2,128)(2,1)} %param.7) | copy-start | bytes 786436
  0.0 23.1 %copy-start.2 = (s32[2048,3]{0,1:T(4,128)S(1)}, s32[2048,3]{0,1:T(4,128)}, u32[]{:S(2)}) copy-start(s32[2048,3]{0,1:T(4,128)} %param.9) | copy-start | bytes 73732
  3.5 39.0 %all-to-all-start = ((bf16[64,2,1024]{2,1,0:T(2,128)(2,1)}), bf16[64,2,1024]{2,1,0:T(2,128)(2,1)S(1)}, u32[]{:S(2)}, u32[]{:S(2)}) async-start(bf16[64,2,1024]{2,1,0:T(2,128)(2,1)} %broadcast_select_fusion.1), calls=%async_computation | async-start | bytes 524288 | tf_op jit(solution)/shard_map/all_to_all | solution.py:181
  44.4 14.3 %all-to-all-start.1 = ((bf16[32,2,2048]{2,1,0:T(2,128)(2,1)}), bf16[32,2,2048]{2,1,0:T(2,128)(2,1)S(1)}, u32[]{:S(2)}, u32[]{:S(2)}) async-start(bf16[32,2,2048]{2,1,0:T(2,128)(2,1)} %pad_maximum_fusion), calls=%async_computation.1 | async-start | bytes 524288 | tf_op jit(solution)/shard_map/all_to_all | solution.py:190
  58.8 0.7 copy-start.1
  67.2 11.4 %all-to-all-start.2 = ((f16[32,2,2176]{2,1,0:T(2,128)(2,1)}), f16[32,2,2176]{2,1,0:T(2,128)(2,1)S(1)}, u32[]{:S(2)}, u32[]{:S(2)}) async-start(f16[32,2,2176]{2,1,0:T(2,128)(2,1)} %convert_element_type.57), calls=%async_computation.2 | async-start | bytes 557056 | tf_op jit(solution)/shard_map/all_to_all | solution.py:200
  81.0 29.7 %all-to-all-start.3 = ((f16[64,2,1152]{2,1,0:T(2,128)(2,1)}), f16[64,2,1152]{2,1,0:T(2,128)(2,1)S(1)}, u32[]{:S(2)}, u32[]{:S(2)}) async-start(f16[64,2,1152]{2,1,0:T(2,128)(2,1)} %broadcast_select_fusion), calls=%async_computation.3 | async-start | bytes 589824 | tf_op jit(solution)/shard_map/all_to_all | solution.py:206
where the time goes:
time: 114 us; the launch traced here: 113 us
  waiting for transfers between devices  48.7 us (43%)
  starting transfers between devices  33.7 us (30%)
  local copies, waits for them, and re-layouts  10.8 us (9%)
  Pallas kernels  9.54 us (8%)
  other arithmetic  9.3 us (8%)
    all_to_all x1, waiting for transfers between devices, per_device(): lax.all_to_all(jnp.take(terms[:, :, :plane + LANES], row_of_slot, axis=0)...  21.8 us
    all_to_all x1, starting transfers between devices, per_device(): lax.all_to_all(jnp.take(orbitals, asked_local, axis=0), 'orb', split_axis...  16.7 us
    all_to_all x1, waiting for transfers between devices, per_device(): lax.all_to_all(jnp.take(orbitals, asked_local, axis=0), 'orb', split_axis...  16.3 us
    all_to_all x1, waiting for transfers between devices, per_device(): lax.all_to_all(terms, 'grp', split_axis=0, concat_axis=0, tiled=True)  7.69 us
    all_to_all x1, starting transfers between devices, per_device(): boxes = lax.all_to_all(rows, 'grp', split_axis=0, concat_axis=0, tiled=True)  6.75 us
    all_to_all x1, starting transfers between devices, per_device(): lax.all_to_all(jnp.take(terms[:, :, :plane + LANES], row_of_slot, axis=0)...  6.48 us
    pallas_call x1, Pallas kernels, pair_terms(): pl.pallas_call(functools.partial(pair_kernel, share), out_shape=jax.Shape...  5.75 us
    pallas_call x1, Pallas kernels, plane_tables(): pl.pallas_call(plane_kernel, out_shape=(shape, shape), name='plane_tables')  3.79 us
  transfers between devices with their start and end apart: 4, of which 4 were waited for; matrix products, arithmetic and copies ran while one was open for 7% of the time, Pallas kernels for 3%

commit v1 on v0

v1 whole, which is shorter than its diff:
```python
import functools
import math

import jax
import jax.numpy as jnp
from jax import lax
from jax.experimental import pallas as pl
from jax.experimental.pallas import tpu as pltpu
from jax.sharding import PartitionSpec as P

BOX = 32
PLANE = BOX * BOX
ORB_GRP = 64
CAP = 2
SCREEN = 0.25
highest = lax.Precision.HIGHEST


def sine_table():
    counts = jnp.arange(BOX).astype(jnp.float32) + 1.0
    return jnp.sqrt(2.0 / (BOX + 1.0)) * jnp.sin(
        math.pi * counts[:, None] * counts[None, :] / (BOX + 1.0)
    )


def green_rows():
    levels = 2.0 - 2.0 * jnp.cos(
        math.pi * (jnp.arange(BOX).astype(jnp.float32) + 1.0) / (BOX + 1.0)
    )
    lanes = jnp.arange(PLANE, dtype=jnp.int32)

    def level(index):
        return 2.0 - 2.0 * jnp.cos(math.pi * (index.astype(jnp.float32) + 1.0) / (BOX + 1.0))

    return 1.0 / (levels[:, None] + (level(lanes // BOX) + level(lanes % BOX))[None, :] + SCREEN)


def halves(value):
    high = value.astype(jnp.bfloat16)
    return high, (value - high.astype(jnp.float32)).astype(jnp.bfloat16)


def dot(a, b):
    return jnp.dot(a, b, preferred_element_type=jnp.float32)


def plane_kernel(sine_ref, high_ref, low_ref):
    lane = lax.broadcasted_iota(jnp.int32, (BOX, PLANE), 1)
    row = lax.broadcasted_iota(jnp.int32, (BOX, PLANE), 0)
    by_y = jnp.where((lane >> 5) == row, 1.0, 0.0).astype(jnp.bfloat16)
    by_z = jnp.where((lane & (BOX - 1)) == row, 1.0, 0.0).astype(jnp.bfloat16)
    sine = sine_ref[...]
    parts = []
    rest = sine
    for _ in range(3):
        piece = rest.astype(jnp.bfloat16)
        parts.append(piece)
        rest = rest - piece.astype(jnp.float32)
    cols_y = dot(parts[0], by_y) + dot(parts[1], by_y) + dot(parts[2], by_y)
    cols_z = dot(parts[0], by_z) + dot(parts[1], by_z) + dot(parts[2], by_z)
    for m in range(BOX):
        block = cols_y[m : m + 1, :] * cols_z
        high = block.astype(jnp.bfloat16)
        high_ref[pl.ds(m * BOX, BOX), :] = high
        low_ref[pl.ds(m * BOX, BOX), :] = (block - high.astype(jnp.float32)).astype(jnp.bfloat16)


def plane_tables(sine):
    shape = jax.ShapeDtypeStruct((PLANE, PLANE), jnp.bfloat16)
    return pl.pallas_call(plane_kernel, out_shape=(shape, shape), name="plane_tables")(sine)


PAIR = 2


def pack_kernel(pattern, from_incoming_ref, from_own_ref, incoming_ref, orbitals_ref, out_ref):
    taken = mine = 0
    for n in range(out_ref.shape[0]):
        if pattern[n % len(pattern)]:
            out_ref[n] = incoming_ref[from_incoming_ref[taken]]
            taken += 1
        else:
            out_ref[n] = orbitals_ref[from_own_ref[mine]]
            mine += 1


def same_pair():
    row = lax.broadcasted_iota(jnp.int32, (PAIR * BOX, PAIR * BOX), 0)
    col = lax.broadcasted_iota(jnp.int32, (PAIR * BOX, PAIR * BOX), 1)
    return row, col, (row >> 5) == (col >> 5)


def steps_along_x(moves_ref, at, back):
    row, col, same = same_pair()
    step = jnp.zeros(row.shape, jnp.int32)
    for k in range(PAIR):
        step = jnp.where((row >> 5) == k, moves_ref[at + k, 0], step)
    hit = (row == col + step) if back else (col == row + step)
    return jnp.where(same & hit, 1.0, 0.0).astype(jnp.bfloat16)


def moved(value, dy, dz):
    lane = lax.broadcasted_iota(jnp.int32, value.shape, 1)
    y, z = lane >> 5, lane & (BOX - 1)
    turned = pltpu.roll(value, (PLANE - (dy * BOX + dz)) & (PLANE - 1), 1)
    inside = (y + dy >= 0) & (y + dy < BOX) & (z + dz >= 0) & (z + dz < BOX)
    return jnp.where(inside, turned, 0.0)


def solve_kernel(
    homes,
    share,
    moves_ref,
    boxes_ref,
    sine_ref,
    green_hbm,
    high_hbm,
    low_hbm,
    out_ref,
    first,
    second,
    held,
    green_ref,
    high_ref,
    low_ref,
    sems,
):
    rows = share * BOX
    depth = boxes_ref.shape[1]
    sides = BOX // depth
    copies = [
        pltpu.make_async_copy(source, into, sems.at[n])
        for n, (source, into) in enumerate(
            ((high_hbm, high_ref), (low_hbm, low_ref), (green_hbm, green_ref))
        )
    ]
    for copy in copies:
        copy.start()
    for s in range(sides):
        for k in range(share):
            at = k * BOX + s * depth
            box = s * 2 * share + k
            first[at : at + depth, :] = boxes_ref[box].astype(jnp.float32)
            second[at : at + depth, :] = boxes_ref[box + share].astype(jnp.float32)

    _, _, same = same_pair()
    wide = jnp.concatenate([jnp.concatenate([sine_ref[...]] * PAIR, 1)] * PAIR, 0)
    sine_high, sine_low = halves(jnp.where(same, wide, 0.0))
    three = jnp.concatenate([sine_high, sine_high, sine_low], 1)

    def along_x(value):
        high, low = halves(value)
        return dot(three, jnp.concatenate([high, low, high], 0))

    def along_plane(value):
        high, low = halves(value)
        both = dot(jnp.concatenate([high, low], 0), high_ref[...])
        return both[:rows] + both[rows:] + dot(high, low_ref[...])

    charges = []
    for at in range(0, share, PAIR):
        turned = [
            moved(second[k * BOX : (k + 1) * BOX, :], moves_ref[k, 1], moves_ref[k, 2])
            for k in range(at, at + PAIR)
        ]
        ahead = steps_along_x(moves_ref, at, False)
        shifted = dot(ahead, jnp.concatenate(turned, 0).astype(jnp.bfloat16))
        part = slice(at * BOX, (at + PAIR) * BOX)
        if at < homes:
            second[part, :] = shifted
        charges.append(along_x(first[part, :] * shifted))
    for copy in copies:
        copy.wait()
    modes = along_plane(jnp.concatenate(charges, 0))
    held[...] = along_plane(modes * jnp.concatenate([green_ref[...]] * share, 0))
    for at in range(0, share, PAIR):
        part = slice(at * BOX, (at + PAIR) * BOX)
        potential = along_x(held[part, :])
        if at < homes:
            held[part, :] = potential * second[part, :]
        else:
            high, low = halves(potential * first[part, :])
            back = steps_along_x(moves_ref, at, True)
            upright = dot(jnp.concatenate([back, back], 1), jnp.concatenate([high, low], 0))
            for k in range(PAIR):
                held[(at + k) * BOX : (at + k + 1) * BOX, :] = moved(
                    upright[k * BOX : (k + 1) * BOX],
                    -moves_ref[at + k, 1],
                    -moves_ref[at + k, 2],
                )
    for s in range(sides):
        for k in range(share):
            at = k * BOX + s * depth
            out_ref[s * share + k] = held[at : at + depth, :]


def take(array, index):
    return array.at[index].get(mode="promise_in_bounds")


VMEM = pl.BlockSpec(memory_space=pltpu.VMEM)
SMEM = pl.BlockSpec(memory_space=pltpu.SMEM)
HBM = pl.BlockSpec(memory_space=pltpu.HBM)
PACK_LIMIT = pltpu.CompilerParams(vmem_limit_bytes=20 << 20)
SOLVE_LIMIT = pltpu.CompilerParams(vmem_limit_bytes=61 << 20)


def packed(pattern, from_incoming, from_own, incoming, orbitals):
    shape = (from_incoming.shape[0] + from_own.shape[0], *orbitals.shape[1:])
    return pl.pallas_call(
        functools.partial(pack_kernel, pattern),
        out_shape=jax.ShapeDtypeStruct(shape, orbitals.dtype),
        in_specs=[SMEM, SMEM, VMEM, VMEM],
        out_specs=VMEM,
        compiler_params=PACK_LIMIT,
        name="pack_rows",
    )(from_incoming, from_own, incoming, orbitals)


def pair_terms(homes, boxes, moves, high, low, green, sine):
    share = moves.shape[0]
    cube = pltpu.VMEM((share * BOX, PLANE), jnp.float32)
    table = pltpu.VMEM((PLANE, PLANE), jnp.bfloat16)
    return pl.pallas_call(
        functools.partial(solve_kernel, homes, share),
        out_shape=jax.ShapeDtypeStruct((boxes.shape[0] // 2, *boxes.shape[1:]), jnp.float32),
        in_specs=[SMEM, VMEM, VMEM, HBM, HBM, HBM],
        out_specs=VMEM,
        scratch_shapes=[
            cube,
            cube,
            cube,
            pltpu.VMEM((BOX, PLANE), jnp.float32),
            table,
            table,
            pltpu.SemaphoreType.DMA((3,)),
        ],
        compiler_params=SOLVE_LIMIT,
        name="pair_terms",
    )(moves, boxes, sine, green, high, low)


def per_device(orbitals, pair_list, offsets):
    groups = lax.axis_size("orb")
    layers = lax.axis_size("grp")
    me = lax.axis_index("orb")
    region = lax.axis_index("grp")
    held, depth, plane = orbitals.shape
    slot_count = groups * CAP
    pair_count = pair_list.shape[1]
    rows_each = pair_count // layers
    slots_each = slot_count // layers
    swap = functools.partial(lax.all_to_all, split_axis=0, concat_axis=0, tiled=True)

    wanted = me * CAP + jnp.arange(CAP, dtype=jnp.int32)
    asked = pair_list[:, None, :, 2] == wanted[None, :, None]
    home_second = jnp.sum(jnp.where(asked, pair_list[:, None, :, 1], 0), axis=2)
    own = lax.dynamic_index_in_dim(pair_list, me, 0, keepdims=False)
    first_local, second_local, slot = own[:, 0], own[:, 1], own[:, 2]
    slot_ids = jnp.arange(slot_count, dtype=jnp.int32)
    named = slot[None, :] == slot_ids[:, None]
    sent_first = jnp.sum(jnp.where(named, first_local[None, :], 0), axis=1).reshape(groups, CAP)
    outgoing = jnp.concatenate([home_second, sent_first], axis=1).reshape(2 * slot_count)
    incoming = swap(take(orbitals, outgoing), "orb")

    home_second = home_second.reshape(slot_count)
    home_valid = jnp.any(asked, axis=2).reshape(slot_count)
    home_first = jnp.sum(jnp.where(asked, pair_list[:, None, :, 0], 0), axis=2).reshape(slot_count)
    from_rows = (slot // CAP * (2 * CAP) + slot % CAP).reshape(layers, rows_each)
    from_slots = (slot_ids // CAP * (2 * CAP) + CAP + slot_ids % CAP).reshape(layers, slots_each)
    pattern = (False,) * slots_each + (True,) * (rows_each + slots_each) + (False,) * rows_each
    from_incoming = jnp.concatenate([from_rows, from_slots], axis=1).reshape(-1)
    from_own = jnp.concatenate(
        [home_second.reshape(layers, slots_each), first_local.reshape(layers, rows_each)], axis=1
    ).reshape(-1)

    def part(values, count):
        return lax.dynamic_slice_in_dim(values, region * count, count, 0)

    first_ids = jnp.concatenate(
        [
            part(slot_ids // CAP * ORB_GRP + home_first, slots_each),
            part(me * ORB_GRP + first_local, rows_each),
        ]
    )
    second_ids = jnp.concatenate(
        [
            part(me * ORB_GRP + home_second, slots_each),
            part(slot // CAP * ORB_GRP + second_local, rows_each),
        ]
    )
    moves = take(offsets, first_ids) - take(offsets, second_ids)
    sine = sine_table()
    high, low = plane_tables(sine)
    green = green_rows()
    target = jnp.concatenate(
        [
            jnp.where(home_valid, home_second, held).reshape(layers, slots_each),
            first_local.reshape(layers, rows_each),
        ],
        axis=1,
    ).reshape(-1)
    hit = jnp.where(target[None, :] == jnp.arange(held, dtype=jnp.int32)[:, None], 1.0, 0.0)
    incoming, from_incoming, from_own, moves, sine, high, low, green, hit = (
        lax.optimization_barrier(
            (incoming, from_incoming, from_own, moves, sine, high, low, green, hit)
        )
    )

    boxes = swap(packed(pattern, from_incoming, from_own, incoming, orbitals), "grp")
    terms = swap(pair_terms(slots_each, boxes, moves, high, low, green, sine), "grp")
    action = jnp.dot(hit, terms.reshape(-1, depth * plane), precision=highest)
    return action.reshape(orbitals.shape)


def solution(mesh):
    return jax.shard_map(
        per_device,
        mesh=mesh,
        in_specs=(P("orb", "grp", None), P(), P()),
        out_specs=P("orb", "grp", None),
        check_vma=False,
    )
```

time: 114 us -> 104 us (0.912)
  blocking collectives: 0 us -> 36.6 us
  waiting for transfers between devices: 48.7 us -> 24 us
  starting transfers between devices: 33.7 us -> 16.7 us
  other arithmetic: 9.3 us -> 3.13 us
  Pallas kernels: 9.54 us -> 12.4 us
  local copies, waits for them, and re-layouts: 10.8 us -> 9.26 us
    all_to_all x0 -> x2, blocking collectives: none -> 36.6 us  [the longest x1 20.4 us: per_device(): swap(packed(pattern, from_incoming, from_own, incoming, orbitals), 'grp')]
    all_to_all x4 -> x1, waiting for transfers between devices: 48.7 us -> 24 us  [per_device(): incoming = swap(take(orbitals, outgoing), 'orb')]
    all_to_all x4 -> x1, starting transfers between devices: 33.7 us -> 16.7 us  [per_device(): incoming = swap(take(orbitals, outgoing), 'orb')]
    pallas_call x1 -> x2, Pallas kernels: 5.75 us -> 8.62 us  [the longest x1 7.92 us: pair_terms(): pl.pallas_call(functools.partial(solve_kernel, homes, share), out_shape=j...]
    select_n x7 -> x5, other arithmetic: 2.55 us -> 0.17 us  [the longest x3 0.16 us: take(): return array.at[index].get(mode='promise_in_bounds')]
    convert_element_type x1 -> x0, other arithmetic: 1.95 us -> none  [per_device(): pair_terms(boxes, moves, high, low, green_rows(), sine).astype(jnp.float16)]
    dot_general x0 -> x1, local copies, waits for them, and re-layouts: none -> 1.2 us  [per_device(): action = jnp.dot(hit, terms.reshape(-1, depth * plane), precision=highest)]
    gather x6 -> x3, local copies, waits for them, and re-layouts: 5.04 us -> 4.45 us  [take(): return array.at[index].get(mode='promise_in_bounds')]
  transfers between devices with their start and end apart: 4 -> 1, of which waited for: 4 -> 1; matrix products, arithmetic and copies ran while one was open for 7% -> 5% of each run, Pallas kernels for 3% -> 4%
where the time goes in v1:
time: 104 us; the launch traced here: 103 us
  blocking collectives  36.6 us (35%)
  waiting for transfers between devices  24 us (23%)
  starting transfers between devices  16.7 us (16%)
  Pallas kernels  12.4 us (12%)
  local copies, waits for them, and re-layouts  9.26 us (9%)
  other arithmetic  3.13 us (3%)
    all_to_all x1, waiting for transfers between devices, per_device(): incoming = swap(take(orbitals, outgoing), 'orb')  24 us
    all_to_all x1, blocking collectives, per_device(): swap(packed(pattern, from_incoming, from_own, incoming, orbitals), 'grp')  20.4 us
    all_to_all x1, starting transfers between devices, per_device(): incoming = swap(take(orbitals, outgoing), 'orb')  16.7 us
    all_to_all x1, blocking collectives, per_device(): swap(pair_terms(slots_each, boxes, moves, high, low, green, sine), 'grp')  16.2 us
    pallas_call x1, Pallas kernels, pair_terms(): pl.pallas_call(functools.partial(solve_kernel, homes, share), out_shape=j...  7.92 us
    gather x3, local copies, waits for them, and re-layouts, take(): return array.at[index].get(mode='promise_in_bounds')  4.45 us
    pallas_call x1, Pallas kernels, plane_tables(): pl.pallas_call(plane_kernel, out_shape=(shape, shape), name='plane_tables')  3.79 us
  transfers between devices with their start and end apart: 1, of which 1 were waited for; matrix products, arithmetic and copies ran while one was open for 5% of the time, Pallas kernels for 4%

profile of v1, /device:TPU:1, one launch (start us, length us, event | category | flops | bytes accessed | tf_op | source)
XLA Modules:
  0.0 103.2 jit_solution(9234741403062035761)
XLA Ops:
  0.0 0.0 copy-start
  0.0 0.0 copy-start.1
  0.0 0.8 slice_bitcast_fusion.1
  0.8 0.7 constant_dynamic-slice_fusion
  1.6 0.1 select_reduce_fusion
  1.6 0.1 reshape.295
  1.8 0.1 copy.19
  1.8 0.2 fusion.4
  2.1 0.1 copy.20
  2.2 0.1 reshape.296
  2.3 3.3 %gather_fusion = bf16[128,2,1024]{2,1,0:T(2,128)(2,1)} fusion(bf16[64,2,1024]{2,1,0:T(2,128)(2,1)} %orbitals_ref.1, s32[1024]{0:T(1024)S(1)} %pad_clamp_fusion.2), kind=kCustom, calls=%fused_computation | custom fusion | bytes 1049088 | tf_op jit(solution)/shard_map/gather | solution.py:198
  5.6 16.7 %all-to-all-start = ((bf16[128,2,1024]{2,1,0:T(2,128)(2,1)}), bf16[128,2,1024]{2,1,0:T(2,128)(2,1)S(1)}, u32[]{:S(2)}, u32[]{:S(2)}) async-start(bf16[128,2,1024]{2,1,0:T(2,128)(2,1)} %gather_fusion), calls=%async_computation | async-start | bytes 1048576 | tf_op jit(solution)/shard_map/all_to_all | solution.py:264
  22.4 0.2 compare_reduce_fusion
  22.6 0.1 copy.21
  22.7 0.1 reshape_squeeze.4
  22.8 0.1 squeeze.12
  22.9 0.1 pad_add_fusion
  23.0 0.1 reshape.297.from_incoming_ref
  23.1 0.1 copy.26
  23.2 0.1 reshape.300
  23.3 0.1 reshape_reshape.3
  23.3 0.1 pad_add_fusion.2
  23.4 0.1 eq.59
  23.5 0.1 reshape.298.from_own_ref
  23.6 0.1 copy.24
  23.7 0.1 add.207
  23.8 0.1 copy.22
  23.9 0.1 reshape.299
  24.0 0.0 copy-done.1
  24.0 0.4 copy.23
  24.4 0.1 dynamic-slice_bitcast_fusion
  24.5 0.1 dynamic-slice_bitcast_fusion.1
  24.6 0.1 fusion.45
  24.7 0.6 gather_fusion.2
  25.2 0.1 fusion.44
  25.3 0.6 gather_fusion.1
  25.9 0.7 sine_multiply_fusion.sine_ref
  26.6 3.8 %plane_tables.1 = (bf16[1024,1024]{1,0:T(8,128)(2,1)}, bf16[1024,1024]{1,0:T(8,128)(2,1)}) custom-call(f32[32,32]{1,0:T(8,128)} %sine_multiply_fusion.sine_ref), custom_call_target="tpu_custom_call" | custom-call | tf_op jit(solution)/shard_map/plane_tables/pallas_call | solution.py:70
  30.4 0.6 sub.54.moves_ref
  31.0 0.1 fusion.33
  31.1 0.7 add_divide_fusion.green_hbm
  31.9 24.0 %all-to-all-done.incoming_ref = bf16[128,2,1024]{2,1,0:T(2,128)(2,1)S(1)} async-done(((bf16[128,2,1024]{2,1,0:T(2,128)(2,1)}), bf16[128,2,1024]{2,1,0:T(2,128)(2,1)S(1)}, u32[]{:S(2)}, u32[]{:S(2)}) %all-to-all-start) | async-done | bytes 524320 | tf_op jit(solution)/shard_map/all_to_all | solution.py:264
  55.9 0.0 copy-done
  55.9 0.7 pack_rows.1
  56.6 20.4 %all_to_all.15.boxes_ref = bf16[192,2,1024]{2,1,0:T(2,128)(2,1)} all-to-all(bf16[192,2,1024]{2,1,0:T(2,128)(2,1)S(1)} %pack_rows.1), channel_id=1, replica_groups=mesh['orb'=32,'grp'=16] {'grp'}, dimensions={0} | all-to-all | bytes 1572864 | tf_op jit(solution)/shard_map/all_to_all | solution.py:310
  77.0 7.9 %pair_terms.1 = f32[96,2,1024]{2,1,0:T(2,128)} custom-call(s32[6,3]{1,0:T(8,128)} %sub.54.moves_ref, bf16[192,2,1024]{2,1,0:T(2,128)(2,1)} %all_to_all.15.boxes_ref, f32[32,32]{1,0:T(8,128)} %sine_multiply_fusion.sine_ref, f32[32,1024]{1,0:T(8,128)} %add_divide_fusion.green_hbm, bf16[1024,1024]{1,0:T(8,128)(2,1)} %get-tuple-element.25.high_hbm, ...), custom_call_target="tpu_custom_call" | custom-call | tf_op jit(solution)/shard_map/pair_terms/pallas_call | solution.py:224
  84.9 16.2 %all_to_all.16 = f32[96,2,1024]{2,1,0:T(2,128)S(1)} all-to-all(f32[96,2,1024]{2,1,0:T(2,128)} %pair_terms.1), channel_id=1, replica_groups=mesh['orb'=32,'grp'=16] {'grp'}, dimensions={0} | all-to-all | bytes 1572864 | tf_op jit(solution)/shard_map/all_to_all | solution.py:311
  101.1 0.8 fusion
  102.0 1.2 %copy.28 = f32[64,2,1024]{2,1,0:T(2,128)} copy(f32[64,2,1024]{2,0,1:T(8,128)S(1)} %fusion) | data formatting | bytes 1048576 | tf_op jit(solution)/shard_map/dot_general | solution.py:312
  (17 shorter events, 0.2 us)
Async XLA Ops:
  0.0 55.9 %copy-start = (bf16[64,2,1024]{2,1,0:T(2,128)(2,1)S(1)}, bf16[64,2,1024]{2,1,0:T(2,128)(2,1)}, u32[]{:S(2)}) copy-start(bf16[64,2,1024]{2,1,0:T(2,128)(2,1)} %orbitals_ref.1) | copy-start | bytes 786436
  0.0 24.0 %copy-start.1 = (s32[2048,3]{0,1:T(4,128)S(1)}, s32[2048,3]{0,1:T(4,128)}, u32[]{:S(2)}) copy-start(s32[2048,3]{0,1:T(4,128)} %param.5) | copy-start | bytes 73732
  5.6 50.3 %all-to-all-start = ((bf16[128,2,1024]{2,1,0:T(2,128)(2,1)}), bf16[128,2,1024]{2,1,0:T(2,128)(2,1)S(1)}, u32[]{:S(2)}, u32[]{:S(2)}) async-start(bf16[128,2,1024]{2,1,0:T(2,128)(2,1)} %gather_fusion), calls=%async_computation | async-start | bytes 1048576 | tf_op jit(solution)/shard_map/all_to_all | solution.py:264

commit v2 on v1

--- a/solution.py
+++ b/solution.py
@@ -13,7 +13,6 @@
 ORB_GRP = 64
 CAP = 2
 SCREEN = 0.25
-highest = lax.Precision.HIGHEST
 
 
 def sine_table():
@@ -44,14 +43,16 @@
     return jnp.dot(a, b, preferred_element_type=jnp.float32)
 
 
-def plane_kernel(sine_ref, high_ref, low_ref):
+TABLES = 10
+
+
+def plane_kernel(sine_ref, tables_hbm, table_ref, sems):
     lane = lax.broadcasted_iota(jnp.int32, (BOX, PLANE), 1)
     row = lax.broadcasted_iota(jnp.int32, (BOX, PLANE), 0)
     by_y = jnp.where((lane >> 5) == row, 1.0, 0.0).astype(jnp.bfloat16)
     by_z = jnp.where((lane & (BOX - 1)) == row, 1.0, 0.0).astype(jnp.bfloat16)
-    sine = sine_ref[...]
     parts = []
-    rest = sine
+    rest = sine_ref[...]
     for _ in range(3):
         piece = rest.astype(jnp.bfloat16)
         parts.append(piece)
@@ -59,29 +60,62 @@
     cols_y = dot(parts[0], by_y) + dot(parts[1], by_y) + dot(parts[2], by_y)
     cols_z = dot(parts[0], by_z) + dot(parts[1], by_z) + dot(parts[2], by_z)
     for m in range(BOX):
-        block = cols_y[m : m + 1, :] * cols_z
-        high = block.astype(jnp.bfloat16)
-        high_ref[pl.ds(m * BOX, BOX), :] = high
-        low_ref[pl.ds(m * BOX, BOX), :] = (block - high.astype(jnp.float32)).astype(jnp.bfloat16)
+        high, low = halves(cols_y[m : m + 1, :] * cols_z)
+        table_ref[0, m * BOX : (m + 1) * BOX, :] = high
+        table_ref[1, m * BOX : (m + 1) * BOX, :] = low
+    copies = [
+        pltpu.make_async_copy(table_ref.at[n], tables_hbm.at[n], sems.at[n]) for n in range(2)
+    ]
+    for copy in copies:
+        copy.start()
+    for copy in copies:
+        copy.wait()
 
 
 def plane_tables(sine):
-    shape = jax.ShapeDtypeStruct((PLANE, PLANE), jnp.bfloat16)
-    return pl.pallas_call(plane_kernel, out_shape=(shape, shape), name="plane_tables")(sine)
+    return pl.pallas_call(
+        plane_kernel,
+        out_shape=jax.ShapeDtypeStruct((TABLES, PLANE, PLANE), jnp.bfloat16),
+        in_specs=[VMEM],
+        out_specs=HBM,
+        scratch_shapes=[
+            pltpu.VMEM((2, PLANE, PLANE), jnp.bfloat16),
+            pltpu.SemaphoreType.DMA((2,)),
+        ],
+        compiler_params=ROWS_LIMIT,
+        name="plane_tables",
+    )(sine)
 
 
 PAIR = 2
 
 
-def pack_kernel(pattern, from_incoming_ref, from_own_ref, incoming_ref, orbitals_ref, out_ref):
+def pick_kernel(sent_ref, kept_ref, orbitals_ref, sent_out, kept_out):
+    for picks_ref, out_ref in ((sent_ref, sent_out), (kept_ref, kept_out)):
+        for n in range(out_ref.shape[0]):
+            out_ref[n] = orbitals_ref[picks_ref[n]]
+
+
+def pack_kernel(pattern, picks_ref, incoming_ref, kept_ref, out_ref):
     taken = mine = 0
     for n in range(out_ref.shape[0]):
         if pattern[n % len(pattern)]:
-            out_ref[n] = incoming_ref[from_incoming_ref[taken]]
+            out_ref[n] = incoming_ref[picks_ref[taken]]
             taken += 1
         else:
-            out_ref[n] = orbitals_ref[from_own_ref[mine]]
+            out_ref[n] = kept_ref[mine]
             mine += 1
+
+
+def sum_kernel(target_ref, weight_ref, terms_ref, out_ref, *sums):
+    sums = (out_ref, *sums)
+    for held in sums:
+        held[...] = jnp.zeros_like(held)
+    for n in range(terms_ref.shape[0]):
+        at = target_ref[n]
+        held = sums[n % len(sums)]
+        held[at] = held[at] + weight_ref[n] * terms_ref[n]
+    out_ref[...] = sum(held[...] for held in sums)
 
 
 def same_pair():
@@ -114,15 +148,13 @@
     boxes_ref,
     sine_ref,
     green_hbm,
-    high_hbm,
-    low_hbm,
+    table_hbm,
     out_ref,
     first,
     second,
     held,
     green_ref,
-    high_ref,
-    low_ref,
+    table_ref,
     sems,
 ):
     rows = share * BOX
@@ -131,7 +163,7 @@
     copies = [
         pltpu.make_async_copy(source, into, sems.at[n])
         for n, (source, into) in enumerate(
-            ((high_hbm, high_ref), (low_hbm, low_ref), (green_hbm, green_ref))
+            ((table_hbm.at[0], table_ref.at[0]), (table_hbm.at[1], table_ref.at[1]), (green_hbm, green_ref))
         )
     ]
     for copy in copies:
@@ -154,8 +186,8 @@
 
     def along_plane(value):
         high, low = halves(value)
-        both = dot(jnp.concatenate([high, low], 0), high_ref[...])
-        return both[:rows] + both[rows:] + dot(high, low_ref[...])
+        both = dot(jnp.concatenate([high, low], 0), table_ref[0])
+        return both[:rows] + both[rows:] + dot(high, table_ref[1])
 
     charges = []
     for at in range(0, share, PAIR):
@@ -169,9 +201,12 @@
         if at < homes:
             second[part, :] = shifted
         charges.append(along_x(first[part, :] * shifted))
-    for copy in copies:
-        copy.wait()
-    modes = along_plane(jnp.concatenate(charges, 0))
+    copies[0].wait()
+    high, low = halves(jnp.concatenate(charges, 0))
+    both = dot(jnp.concatenate([high, low], 0), table_ref[0])
+    copies[1].wait()
+    modes = both[:rows] + both[rows:] + dot(high, table_ref[1])
+    copies[2].wait()
     held[...] = along_plane(modes * jnp.concatenate([green_ref[...]] * share, 0))
     for at in range(0, share, PAIR):
         part = slice(at * BOX, (at + PAIR) * BOX)
@@ -201,43 +236,68 @@
 VMEM = pl.BlockSpec(memory_space=pltpu.VMEM)
 SMEM = pl.BlockSpec(memory_space=pltpu.SMEM)
 HBM = pl.BlockSpec(memory_space=pltpu.HBM)
-PACK_LIMIT = pltpu.CompilerParams(vmem_limit_bytes=20 << 20)
-SOLVE_LIMIT = pltpu.CompilerParams(vmem_limit_bytes=61 << 20)
-
-
-def packed(pattern, from_incoming, from_own, incoming, orbitals):
-    shape = (from_incoming.shape[0] + from_own.shape[0], *orbitals.shape[1:])
+ROWS_LIMIT = pltpu.CompilerParams(vmem_limit_bytes=20 << 20)
+SOLVE_LIMIT = pltpu.CompilerParams(vmem_limit_bytes=46 << 20)
+
+
+def picked(sent, kept, orbitals):
+    return pl.pallas_call(
+        pick_kernel,
+        out_shape=tuple(
+            jax.ShapeDtypeStruct((n.shape[0], *orbitals.shape[1:]), orbitals.dtype)
+            for n in (sent, kept)
+        ),
+        in_specs=[SMEM, SMEM, VMEM],
+        out_specs=(VMEM, VMEM),
+        compiler_params=ROWS_LIMIT,
+        name="pick_rows",
+    )(sent, kept, orbitals)
+
+
+def summed(target, weight, terms, held):
+    return pl.pallas_call(
+        sum_kernel,
+        out_shape=jax.ShapeDtypeStruct((held, *terms.shape[1:]), terms.dtype),
+        in_specs=[SMEM, SMEM, VMEM],
+        out_specs=VMEM,
+        scratch_shapes=[pltpu.VMEM((held, *terms.shape[1:]), terms.dtype)] * 3,
+        compiler_params=ROWS_LIMIT,
+        name="sum_rows",
+    )(target, weight, terms)
+
+
+def packed(pattern, picks, incoming, kept):
+    shape = (picks.shape[0] + kept.shape[0], *kept.shape[1:])
     return pl.pallas_call(
         functools.partial(pack_kernel, pattern),
-        out_shape=jax.ShapeDtypeStruct(shape, orbitals.dtype),
-        in_specs=[SMEM, SMEM, VMEM, VMEM],
+        out_shape=jax.ShapeDtypeStruct(shape, kept.dtype),
+        in_specs=[SMEM, VMEM, VMEM],
         out_specs=VMEM,
-        compiler_params=PACK_LIMIT,
+        compiler_params=ROWS_LIMIT,
         name="pack_rows",
-    )(from_incoming, from_own, incoming, orbitals)
-
-
-def pair_terms(homes, boxes, moves, high, low, green, sine):
+    )(picks, incoming, kept)
+
+
+def pair_terms(homes, boxes, moves, table, green, sine):
     share = moves.shape[0]
     cube = pltpu.VMEM((share * BOX, PLANE), jnp.float32)
-    table = pltpu.VMEM((PLANE, PLANE), jnp.bfloat16)
+    halves_type = pltpu.VMEM((2, PLANE, PLANE), jnp.bfloat16)
     return pl.pallas_call(
         functools.partial(solve_kernel, homes, share),
         out_shape=jax.ShapeDtypeStruct((boxes.shape[0] // 2, *boxes.shape[1:]), jnp.float32),
-        in_specs=[SMEM, VMEM, VMEM, HBM, HBM, HBM],
+        in_specs=[SMEM, VMEM, VMEM, HBM, HBM],
         out_specs=VMEM,
         scratch_shapes=[
             cube,
             cube,
             cube,
             pltpu.VMEM((BOX, PLANE), jnp.float32),
-            table,
-            table,
+            halves_type,
             pltpu.SemaphoreType.DMA((3,)),
         ],
         compiler_params=SOLVE_LIMIT,
         name="pair_terms",
-    )(moves, boxes, sine, green, high, low)
+    )(moves, boxes, sine, green, table)
 
 
 def per_device(orbitals, pair_list, offsets):
@@ -252,27 +312,31 @@
     slots_each = slot_count // layers
     swap = functools.partial(lax.all_to_all, split_axis=0, concat_axis=0, tiled=True)
 
+    pair_list = lax.optimization_barrier(tuple(pair_list[:, :, n] for n in range(3)))
+    is_me = jnp.arange(groups, dtype=jnp.int32)[:, None] == me
+    first_local, second_local, slot = (
+        jnp.sum(jnp.where(is_me, plane_of, 0), axis=0) for plane_of in pair_list
+    )
     wanted = me * CAP + jnp.arange(CAP, dtype=jnp.int32)
-    asked = pair_list[:, None, :, 2] == wanted[None, :, None]
-    home_second = jnp.sum(jnp.where(asked, pair_list[:, None, :, 1], 0), axis=2)
-    own = lax.dynamic_index_in_dim(pair_list, me, 0, keepdims=False)
-    first_local, second_local, slot = own[:, 0], own[:, 1], own[:, 2]
+    asked = pair_list[2][:, None, :] == wanted[None, :, None]
+    home_second = jnp.sum(jnp.where(asked, pair_list[1][:, None, :], 0), axis=2)
     slot_ids = jnp.arange(slot_count, dtype=jnp.int32)
     named = slot[None, :] == slot_ids[:, None]
     sent_first = jnp.sum(jnp.where(named, first_local[None, :], 0), axis=1).reshape(groups, CAP)
     outgoing = jnp.concatenate([home_second, sent_first], axis=1).reshape(2 * slot_count)
-    incoming = swap(take(orbitals, outgoing), "orb")
+    local = jnp.concatenate(
+        [home_second.reshape(layers, slots_each), first_local.reshape(layers, rows_each)], axis=1
+    ).reshape(-1)
+    outgoing, kept = picked(outgoing, local, orbitals)
+    incoming = swap(outgoing, "orb")
 
     home_second = home_second.reshape(slot_count)
     home_valid = jnp.any(asked, axis=2).reshape(slot_count)
-    home_first = jnp.sum(jnp.where(asked, pair_list[:, None, :, 0], 0), axis=2).reshape(slot_count)
+    home_first = jnp.sum(jnp.where(asked, pair_list[0][:, None, :], 0), axis=2).reshape(slot_count)
     from_rows = (slot // CAP * (2 * CAP) + slot % CAP).reshape(layers, rows_each)
     from_slots = (slot_ids // CAP * (2 * CAP) + CAP + slot_ids % CAP).reshape(layers, slots_each)
     pattern = (False,) * slots_each + (True,) * (rows_each + slots_each) + (False,) * rows_each
     from_incoming = jnp.concatenate([from_rows, from_slots], axis=1).reshape(-1)
-    from_own = jnp.concatenate(
-        [home_second.reshape(layers, slots_each), first_local.reshape(layers, rows_each)], axis=1
-    ).reshape(-1)
 
     def part(values, count):
         return lax.dynamic_slice_in_dim(values, region * count, count, 0)
@@ -291,26 +355,24 @@
     )
     moves = take(offsets, first_ids) - take(offsets, second_ids)
     sine = sine_table()
-    high, low = plane_tables(sine)
+    table = plane_tables(sine)
     green = green_rows()
-    target = jnp.concatenate(
+    weight = jnp.concatenate(
         [
-            jnp.where(home_valid, home_second, held).reshape(layers, slots_each),
-            first_local.reshape(layers, rows_each),
+            jnp.where(home_valid, 1.0, 0.0).reshape(layers, slots_each),
+            jnp.ones((layers, rows_each), jnp.float32),
         ],
         axis=1,
     ).reshape(-1)
-    hit = jnp.where(target[None, :] == jnp.arange(held, dtype=jnp.int32)[:, None], 1.0, 0.0)
-    incoming, from_incoming, from_own, moves, sine, high, low, green, hit = (
+    incoming, from_incoming, kept, moves, sine, table, green, local, weight = (
         lax.optimization_barrier(
-            (incoming, from_incoming, from_own, moves, sine, high, low, green, hit)
+            (incoming, from_incoming, kept, moves, sine, table, green, local, weight)
         )
     )
 
-    boxes = swap(packed(pattern, from_incoming, from_own, incoming, orbitals), "grp")
-    terms = swap(pair_terms(slots_each, boxes, moves, high, low, green, sine), "grp")
-    action = jnp.dot(hit, terms.reshape(-1, depth * plane), precision=highest)
-    return action.reshape(orbitals.shape)
+    boxes = swap(packed(pattern, from_incoming, incoming, kept), "grp")
+    terms = swap(pair_terms(slots_each, boxes, moves, table, green, sine), "grp")
+    return summed(local, weight, terms, held)
 
 
 def solution(mesh):

time: 104 us -> 99.5 us (0.957)
  local copies, waits for them, and re-layouts: 9.26 us -> 12.7 us
  waiting for transfers between devices: 24 us -> 20.8 us
  other arithmetic: 3.13 us -> 1.36 us
  Pallas kernels: 12.4 us -> 11.1 us
    unnamed x6 -> x5, local copies, waits for them, and re-layouts: 0.37 us -> 9.04 us
    gather x3 -> x2, local copies, waits for them, and re-layouts: 4.45 us -> 1.11 us  [take(): return array.at[index].get(mode='promise_in_bounds')]
    all_to_all x1, waiting for transfers between devices: 24 us -> 20.8 us  [per_device(): incoming = swap(outgoing, 'orb')]
    pallas_call x1, Pallas kernels: 7.92 us -> 5.7 us  [pair_terms(): pl.pallas_call(functools.partial(solve_kernel, homes, share), out_shape=j...]
    dot_general x1 -> x0, local copies, waits for them, and re-layouts: 1.2 us -> none  [per_device(): action = jnp.dot(hit, terms.reshape(-1, depth * plane), precision=highest)]
    pallas_call x1 -> x3, Pallas kernels: 3.79 us -> 4.75 us  [the longest x1 1.75 us: summed(): pl.pallas_call(sum_kernel, out_shape=jax.ShapeDtypeStruct((held, *terms.s...]
  transfers between devices with their start and end apart: 1 -> 1, of which waited for: 1 -> 1; matrix products, arithmetic and copies ran while one was open for 5% -> 4% of each run, Pallas kernels for 4% -> 1%
where the time goes in v2:
time: 99.5 us; the launch traced here: 98.9 us
  blocking collectives  36 us (36%)
  waiting for transfers between devices  20.8 us (21%)
  starting transfers between devices  16.7 us (17%)
  local copies, waits for them, and re-layouts  12.7 us (13%)
  Pallas kernels  11.1 us (11%)
  other arithmetic  1.36 us (1%)
    all_to_all x1, waiting for transfers between devices, per_device(): incoming = swap(outgoing, 'orb')  20.8 us
    all_to_all x1, blocking collectives, per_device(): boxes = swap(packed(pattern, from_incoming, incoming, kept), 'grp')  20.3 us
    all_to_all x1, starting transfers between devices, per_device(): incoming = swap(outgoing, 'orb')  16.7 us
    all_to_all x1, blocking collectives, per_device(): swap(pair_terms(slots_each, boxes, moves, table, green, sine), 'grp')  15.8 us
    unnamed x5, local copies, waits for them, and re-layouts  9.04 us
    pallas_call x1, Pallas kernels, pair_terms(): pl.pallas_call(functools.partial(solve_kernel, homes, share), out_shape=j...  5.7 us
  transfers between devices with their start and end apart: 1, of which 1 were waited for; matrix products, arithmetic and copies ran while one was open for 4% of the time, Pallas kernels for 1%

profile of v2, /device:TPU:1, one launch (start us, length us, event | category | flops | bytes accessed | tf_op | source)
XLA Modules:
  0.0 98.9 jit_solution(8192352009324849427)
XLA Ops:
  0.0 0.8 slice_bitcast_fusion
  0.8 0.1 select_reduce_fusion
  0.9 0.2 fusion.1
  1.1 0.1 reshape.278
  1.2 0.1 select_reduce_fusion.1
  1.3 0.1 reshape.275
  1.4 0.1 copy.14
  1.5 0.1 copy.16
  1.6 0.1 copy.15
  1.6 0.1 reshape.276.sent_ref
  1.8 0.1 reshape.277
  1.8 0.1 pad_add_fusion
  1.9 0.1 reshape.279.kept_ref.target_ref
  2.0 0.0 copy-start.1
  2.0 0.9 copy-done.1
  3.0 1.5 %pick_rows.1 = (bf16[128,2,1024]{2,1,0:T(2,128)(2,1)}, bf16[96,2,1024]{2,1,0:T(2,128)(2,1)S(1)}) custom-call(s32[128]{0:T(128)S(1)} %reshape.276.sent_ref, s32[96]{0:T(128)S(1)} %reshape.279.kept_ref.target_ref, bf16[64,2,1024]{2,1,0:T(2,128)(2,1)S(1)} %copy-done.1), custom_call_target="tpu_custom_call" | custom-call | tf_op jit(solution)/shard_map/pick_rows/pallas_call | solution.py:244
  4.5 16.7 %all-to-all-start = ((bf16[128,2,1024]{2,1,0:T(2,128)(2,1)}), bf16[128,2,1024]{2,1,0:T(2,128)(2,1)S(1)}, u32[]{:S(2)}, u32[]{:S(2)}) async-start(bf16[128,2,1024]{2,1,0:T(2,128)(2,1)} %get-tuple-element.22), calls=%async_computation | async-start | bytes 1048576 | tf_op jit(solution)/shard_map/all_to_all | solution.py:331
  21.2 0.2 compare_reduce_fusion
  21.4 0.1 reduce_sum.60
  21.6 0.1 pad_add_fusion.1
  21.6 0.1 reshape.280.picks_ref
  21.7 0.1 copy.19
  21.8 0.1 add.189
  21.9 0.1 copy.17
  22.0 0.1 reshape.281
  22.1 0.1 copy.21
  22.2 0.1 select_n.128
  22.3 0.1 reshape.282.weight_ref
  22.4 1.1 %copy.18 = s32[2048,3]{1,0:T(8,128)S(1)} copy(s32[2048,3]{0,1:T(4,128)} %param.5) | data formatting | bytes 49152 | tf_op args[2]
  23.5 0.1 dynamic-slice_bitcast_fusion
  23.6 0.1 dynamic-slice_bitcast_fusion.1
  23.7 0.1 fusion.39
  23.8 0.6 gather_fusion.1
  24.3 0.1 dynamic-slice_bitcast_fusion.2
  24.4 0.1 fusion.38
  24.5 0.6 gather_fusion
  25.1 0.1 sine_multiply_fusion.sine_ref
  25.2 1.5 %plane_tables.1.table_hbm = bf16[10,1024,1024]{2,1,0:T(8,128)(2,1)S(1)} custom-call(f32[32,32]{1,0:T(8,128)S(1)} %sine_multiply_fusion.sine_ref), custom_call_target="tpu_custom_call" | custom-call | tf_op jit(solution)/shard_map/plane_tables/pallas_call | solution.py:76
  26.7 0.0 copy-start
  26.7 7.0 %copy-done = bf16[10,1024,1024]{2,1,0:T(8,128)(2,1)} copy-done((bf16[10,1024,1024]{2,1,0:T(8,128)(2,1)}, bf16[10,1024,1024]{2,1,0:T(8,128)(2,1)S(1)}, u32[]{:S(2)}) %copy-start) | copy-done | bytes 20971544
  33.7 0.1 fusion.28
  33.8 0.1 add_divide_fusion.green_hbm
  33.9 20.8 %all-to-all-done.incoming_ref = bf16[128,2,1024]{2,1,0:T(2,128)(2,1)S(1)} async-done(((bf16[128,2,1024]{2,1,0:T(2,128)(2,1)}), bf16[128,2,1024]{2,1,0:T(2,128)(2,1)S(1)}, u32[]{:S(2)}, u32[]{:S(2)}) %all-to-all-start) | async-done | bytes 524320 | tf_op jit(solution)/shard_map/all_to_all | solution.py:331
  54.7 0.6 pack_rows.1
  55.4 20.3 %all_to_all.15.boxes_ref = bf16[192,2,1024]{2,1,0:T(2,128)(2,1)S(1)} all-to-all(bf16[192,2,1024]{2,1,0:T(2,128)(2,1)S(1)} %pack_rows.1), channel_id=1, replica_groups=mesh['orb'=32,'grp'=16] {'grp'}, dimensions={0} | all-to-all | bytes 1572864 | tf_op jit(solution)/shard_map/all_to_all | solution.py:373
  75.6 5.7 %pair_terms.1 = f32[96,2,1024]{2,1,0:T(2,128)S(1)} custom-call(s32[6,3]{1,0:T(8,128)S(1)} %sub.54.moves_ref, bf16[192,2,1024]{2,1,0:T(2,128)(2,1)S(1)} %all_to_all.15.boxes_ref, f32[32,32]{1,0:T(8,128)S(1)} %sine_multiply_fusion.sine_ref, f32[32,1024]{1,0:T(8,128)S(1)} %add_divide_fusion.green_hbm, bf16[10,1024,1024]{2,1,0:T(8,128)(2,1)} %copy-done), custom_call_target="tpu_custom_call" | custom-call | tf_op jit(solution)/shard_map/pair_terms/pallas_call | solution.py:285
  81.3 15.8 %all_to_all.16.terms_ref = f32[96,2,1024]{2,1,0:T(2,128)S(1)} all-to-all(f32[96,2,1024]{2,1,0:T(2,128)S(1)} %pair_terms.1), channel_id=1, replica_groups=mesh['orb'=32,'grp'=16] {'grp'}, dimensions={0} | all-to-all | bytes 1572864 | tf_op jit(solution)/shard_map/all_to_all | solution.py:374
  97.1 1.8 %sum_rows.1 = f32[64,2,1024]{2,1,0:T(2,128)} custom-call(s32[96]{0:T(128)S(1)} %reshape.279.kept_ref.target_ref, f32[96]{0:T(128)S(1)} %reshape.282.weight_ref, f32[96,2,1024]{2,1,0:T(2,128)S(1)} %all_to_all.16.terms_ref), custom_call_target="tpu_custom_call" | custom-call | tf_op jit(solution)/shard_map/sum_rows/pallas_call | solution.py:258
  (15 shorter events, 0.2 us)
Async XLA Ops:
  2.0 1.0 copy-start.1
  4.5 50.3 %all-to-all-start = ((bf16[128,2,1024]{2,1,0:T(2,128)(2,1)}), bf16[128,2,1024]{2,1,0:T(2,128)(2,1)S(1)}, u32[]{:S(2)}, u32[]{:S(2)}) async-start(bf16[128,2,1024]{2,1,0:T(2,128)(2,1)} %get-tuple-element.22), calls=%async_computation | async-start | bytes 1048576 | tf_op jit(solution)/shard_map/all_to_all | solution.py:331
  26.7 7.0 %copy-start = (bf16[10,1024,1024]{2,1,0:T(8,128)(2,1)}, bf16[10,1024,1024]{2,1,0:T(8,128)(2,1)S(1)}, u32[]{:S(2)}) copy-start(bf16[10,1024,1024]{2,1,0:T(8,128)(2,1)S(1)} %plane_tables.1.table_hbm) | copy-start | bytes 62914564

commit v3 on v2

--- a/solution.py
+++ b/solution.py
@@ -82,29 +82,48 @@
             pltpu.VMEM((2, PLANE, PLANE), jnp.bfloat16),
             pltpu.SemaphoreType.DMA((2,)),
         ],
-        compiler_params=ROWS_LIMIT,
+        compiler_params=SOLVE_LIMIT,
         name="plane_tables",
     )(sine)
 
 
+SIDE = 4
 PAIR = 2
 
 
-def pick_kernel(sent_ref, kept_ref, orbitals_ref, sent_out, kept_out):
-    for picks_ref, out_ref in ((sent_ref, sent_out), (kept_ref, kept_out)):
-        for n in range(out_ref.shape[0]):
-            out_ref[n] = orbitals_ref[picks_ref[n]]
-
-
-def pack_kernel(pattern, picks_ref, incoming_ref, kept_ref, out_ref):
-    taken = mine = 0
+def pick_kernel(each, place_ref, sent_ref, local_ref, orbitals_ref, sent_out, *local_outs):
+    for n in range(sent_out.shape[0]):
+        sent_out[n] = orbitals_ref[sent_ref[n]]
+    for step, out_ref in enumerate(local_outs):
+        side = (place_ref[1] + step) & (SIDE - 1)
+        for other in range(SIDE):
+            for q in range(each):
+                pick = local_ref[(other * SIDE + side) * each + q]
+                out_ref[other * each + q] = orbitals_ref[pick]
+
+
+def turn_kernel(each, place_ref, *refs):
+    came, gone = refs[:SIDE], refs[SIDE:]
+    for step, out_ref in enumerate(gone):
+        other = (place_ref[0] + step) & (SIDE - 1)
+        for n, in_ref in enumerate(came):
+            for q in range(each):
+                out_ref[n * each + q] = in_ref[other * each + q]
+
+
+def settle_kernel(each, place_ref, *refs):
+    came, out_ref = refs[:SIDE], refs[SIDE]
+    for far, in_ref in enumerate(came):
+        y = (place_ref[0] - far) & (SIDE - 1)
+        for near in range(SIDE):
+            side = y * SIDE + ((place_ref[1] - near) & (SIDE - 1))
+            for q in range(each):
+                out_ref[side * each + q] = in_ref[near * each + q]
+
+
+def pack_kernel(picks_ref, incoming_ref, out_ref):
     for n in range(out_ref.shape[0]):
-        if pattern[n % len(pattern)]:
-            out_ref[n] = incoming_ref[picks_ref[taken]]
-            taken += 1
-        else:
-            out_ref[n] = kept_ref[mine]
-            mine += 1
+        out_ref[n] = incoming_ref[picks_ref[n]]
 
 
 def sum_kernel(target_ref, weight_ref, terms_ref, out_ref, *sums):
@@ -128,7 +147,7 @@
     row, col, same = same_pair()
     step = jnp.zeros(row.shape, jnp.int32)
     for k in range(PAIR):
-        step = jnp.where((row >> 5) == k, moves_ref[at + k, 0], step)
+        step = jnp.where((row >> 5) == k, moves_ref[3 * (at + k)], step)
     hit = (row == col + step) if back else (col == row + step)
     return jnp.where(same & hit, 1.0, 0.0).astype(jnp.bfloat16)
 
@@ -146,6 +165,7 @@
     share,
     moves_ref,
     boxes_ref,
+    local_ref,
     sine_ref,
     green_hbm,
     table_hbm,
@@ -171,9 +191,11 @@
     for s in range(sides):
         for k in range(share):
             at = k * BOX + s * depth
-            box = s * 2 * share + k
-            first[at : at + depth, :] = boxes_ref[box].astype(jnp.float32)
-            second[at : at + depth, :] = boxes_ref[box + share].astype(jnp.float32)
+            mine = second if k < homes else first
+            q = s * share + (share - homes + k if k < homes else k - homes)
+            mine[at : at + depth, :] = boxes_ref[q].astype(jnp.float32)
+            other = first if k < homes else second
+            other[at : at + depth, :] = local_ref[s * share + k].astype(jnp.float32)
 
     _, _, same = same_pair()
     wide = jnp.concatenate([jnp.concatenate([sine_ref[...]] * PAIR, 1)] * PAIR, 0)
@@ -192,7 +214,7 @@
     charges = []
     for at in range(0, share, PAIR):
         turned = [
-            moved(second[k * BOX : (k + 1) * BOX, :], moves_ref[k, 1], moves_ref[k, 2])
+            moved(second[k * BOX : (k + 1) * BOX, :], moves_ref[3 * k + 1], moves_ref[3 * k + 2])
             for k in range(at, at + PAIR)
         ]
         ahead = steps_along_x(moves_ref, at, False)
@@ -220,8 +242,8 @@
             for k in range(PAIR):
                 held[(at + k) * BOX : (at + k + 1) * BOX, :] = moved(
                     upright[k * BOX : (k + 1) * BOX],
-                    -moves_ref[at + k, 1],
-                    -moves_ref[at + k, 2],
+                    -moves_ref[3 * (at + k) + 1],
+                    -moves_ref[3 * (at + k) + 2],
                 )
     for s in range(sides):
         for k in range(share):
@@ -229,10 +251,6 @@
             out_ref[s * share + k] = held[at : at + depth, :]
 
 
-def take(array, index):
-    return array.at[index].get(mode="promise_in_bounds")
-
-
 VMEM = pl.BlockSpec(memory_space=pltpu.VMEM)
 SMEM = pl.BlockSpec(memory_space=pltpu.SMEM)
 HBM = pl.BlockSpec(memory_space=pltpu.HBM)
@@ -240,18 +258,25 @@
 SOLVE_LIMIT = pltpu.CompilerParams(vmem_limit_bytes=46 << 20)
 
 
-def picked(sent, kept, orbitals):
+def rows_call(kernel, name, counts, in_specs, box, *args):
+    out = tuple(jax.ShapeDtypeStruct((n, *box.shape[1:]), box.dtype) for n in counts)
     return pl.pallas_call(
-        pick_kernel,
-        out_shape=tuple(
-            jax.ShapeDtypeStruct((n.shape[0], *orbitals.shape[1:]), orbitals.dtype)
-            for n in (sent, kept)
-        ),
-        in_specs=[SMEM, SMEM, VMEM],
-        out_specs=(VMEM, VMEM),
+        kernel,
+        out_shape=out,
+        in_specs=in_specs,
+        out_specs=(VMEM,) * len(out),
         compiler_params=ROWS_LIMIT,
-        name="pick_rows",
-    )(sent, kept, orbitals)
+        name=name,
+    )(*args)
+
+
+def along(array, step, axis):
+    pairs = []
+    for n in range(SIDE * SIDE):
+        at = list(divmod(n, SIDE))
+        at[axis] = (at[axis] + step) % SIDE
+        pairs.append((n, at[0] * SIDE + at[1]))
+    return lax.ppermute(array, "grp", pairs)
 
 
 def summed(target, weight, terms, held):
@@ -266,26 +291,14 @@
     )(target, weight, terms)
 
 
-def packed(pattern, picks, incoming, kept):
-    shape = (picks.shape[0] + kept.shape[0], *kept.shape[1:])
-    return pl.pallas_call(
-        functools.partial(pack_kernel, pattern),
-        out_shape=jax.ShapeDtypeStruct(shape, kept.dtype),
-        in_specs=[SMEM, VMEM, VMEM],
-        out_specs=VMEM,
-        compiler_params=ROWS_LIMIT,
-        name="pack_rows",
-    )(picks, incoming, kept)
-
-
-def pair_terms(homes, boxes, moves, table, green, sine):
-    share = moves.shape[0]
+def pair_terms(homes, boxes, local, moves, table, green, sine):
+    share = moves.shape[0] // 3
     cube = pltpu.VMEM((share * BOX, PLANE), jnp.float32)
     halves_type = pltpu.VMEM((2, PLANE, PLANE), jnp.bfloat16)
     return pl.pallas_call(
         functools.partial(solve_kernel, homes, share),
-        out_shape=jax.ShapeDtypeStruct((boxes.shape[0] // 2, *boxes.shape[1:]), jnp.float32),
-        in_specs=[SMEM, VMEM, VMEM, HBM, HBM],
+        out_shape=jax.ShapeDtypeStruct(boxes.shape, jnp.float32),
+        in_specs=[SMEM, VMEM, VMEM, VMEM, HBM, HBM],
         out_specs=VMEM,
         scratch_shapes=[
             cube,
@@ -297,7 +310,7 @@
         ],
         compiler_params=SOLVE_LIMIT,
         name="pair_terms",
-    )(moves, boxes, sine, green, table)
+    )(moves, boxes, local, sine, green, table)
 
 
 def per_device(orbitals, pair_list, offsets):
@@ -327,15 +340,48 @@
     local = jnp.concatenate(
         [home_second.reshape(layers, slots_each), first_local.reshape(layers, rows_each)], axis=1
     ).reshape(-1)
-    outgoing, kept = picked(outgoing, local, orbitals)
+    each = rows_each + slots_each
+    side_rows = SIDE * each
+    place = jnp.stack([region // SIDE, region % SIDE])
+    outgoing, *local_rows = rows_call(
+        functools.partial(pick_kernel, each),
+        "pick_rows",
+        (2 * slot_count,) + (side_rows,) * SIDE,
+        [SMEM, SMEM, SMEM, VMEM],
+        orbitals,
+        place,
+        outgoing,
+        local,
+        orbitals,
+    )
     incoming = swap(outgoing, "orb")
+
+    came = [local_rows[0]] + [along(local_rows[n], n, 1) for n in range(1, SIDE)]
+    turned = rows_call(
+        functools.partial(turn_kernel, each),
+        "turn_rows",
+        (side_rows,) * SIDE,
+        [SMEM] + [VMEM] * SIDE,
+        orbitals,
+        place,
+        *came,
+    )
+    (whole,) = rows_call(
+        functools.partial(settle_kernel, each),
+        "settle_rows",
+        (layers * each,),
+        [SMEM] + [VMEM] * SIDE,
+        orbitals,
+        place,
+        turned[0],
+        *(along(turned[n], n, 0) for n in range(1, SIDE)),
+    )
 
     home_second = home_second.reshape(slot_count)
     home_valid = jnp.any(asked, axis=2).reshape(slot_count)
     home_first = jnp.sum(jnp.where(asked, pair_list[0][:, None, :], 0), axis=2).reshape(slot_count)
     from_rows = (slot // CAP * (2 * CAP) + slot % CAP).reshape(layers, rows_each)
     from_slots = (slot_ids // CAP * (2 * CAP) + CAP + slot_ids % CAP).reshape(layers, slots_each)
-    pattern = (False,) * slots_each + (True,) * (rows_each + slots_each) + (False,) * rows_each
     from_incoming = jnp.concatenate([from_rows, from_slots], axis=1).reshape(-1)
 
     def part(values, count):
@@ -353,7 +399,11 @@
             part(slot // CAP * ORB_GRP + second_local, rows_each),
         ]
     )
-    moves = take(offsets, first_ids) - take(offsets, second_ids)
+    ids = jnp.arange(offsets.shape[0], dtype=jnp.int32)
+    signs = (first_ids[:, None] == ids).astype(jnp.int32) - (
+        second_ids[:, None] == ids
+    ).astype(jnp.int32)
+    moves = jnp.sum(signs[:, None, :] * offsets.T[None, :, :], axis=2).reshape(-1)
     sine = sine_table()
     table = plane_tables(sine)
     green = green_rows()
@@ -364,14 +414,24 @@
         ],
         axis=1,
     ).reshape(-1)
-    incoming, from_incoming, kept, moves, sine, table, green, local, weight = (
+    incoming, from_incoming, whole, moves, sine, table, green, local, weight = (
         lax.optimization_barrier(
-            (incoming, from_incoming, kept, moves, sine, table, green, local, weight)
+            (incoming, from_incoming, whole, moves, sine, table, green, local, weight)
         )
     )
 
-    boxes = swap(packed(pattern, from_incoming, incoming, kept), "grp")
-    terms = swap(pair_terms(slots_each, boxes, moves, table, green, sine), "grp")
+    (boxes,) = rows_call(
+        pack_kernel,
+        "pack_rows",
+        (layers * each,),
+        [SMEM, VMEM],
+        orbitals,
+        from_incoming,
+        incoming,
+    )
+    boxes = swap(boxes, "grp")
+    terms = pair_terms(slots_each, boxes, whole, moves, table, green, sine)
+    terms = swap(terms, "grp")
     return summed(local, weight, terms, held)
 
 

time: 99.5 us -> 95.3 us (0.958)
  starting transfers between devices: 16.7 us -> 38 us
  waiting for transfers between devices: 20.8 us -> 4.71 us
  local copies, waits for them, and re-layouts: 12.7 us -> 3.71 us
  blocking collectives: 36 us -> 31.4 us
  Pallas kernels: 11.1 us -> 13.8 us
  other arithmetic: 1.36 us -> 2.41 us
    ppermute x0 -> x6, starting transfers between devices: none -> 21.3 us  [along(): return lax.ppermute(array, 'grp', pairs)]
    all_to_all x1, waiting for transfers between devices: 20.8 us -> 4.23 us  [per_device(): incoming = swap(outgoing, 'orb')]
    unnamed x5 -> x2, local copies, waits for them, and re-layouts: 9.04 us -> 0.95 us
    all_to_all x2, blocking collectives: 36 us -> 31.4 us  [the longest x1 16 us: per_device(): boxes = swap(boxes, 'grp')]
    pallas_call x1, Pallas kernels: 1.48 us -> 3.1 us  [plane_tables(): pl.pallas_call(plane_kernel, out_shape=jax.ShapeDtypeStruct((TABLES, PLAN...]
    pallas_call x2 -> x4, Pallas kernels: 2.14 us -> 3.32 us  [rows_call(): pl.pallas_call(kernel, out_shape=out, in_specs=in_specs, out_specs=(VMEM,...]
    gather x2 -> x0, local copies, waits for them, and re-layouts: 1.11 us -> none  [take(): return array.at[index].get(mode='promise_in_bounds')]
  transfers between devices with their start and end apart: 1 -> 7, of which waited for: 1 -> 2; matrix products, arithmetic and copies ran while one was open for 4% -> 3% of each run, Pallas kernels for 1% -> 5%
where the time goes in v3:
time: 95.3 us; the launch traced here: 94.3 us
  starting transfers between devices  38 us (40%)
  blocking collectives  31.4 us (33%)
  Pallas kernels  13.8 us (14%)
  waiting for transfers between devices  4.71 us (5%)
  local copies, waits for them, and re-layouts  3.71 us (4%)
  other arithmetic  2.41 us (3%)
    ppermute x6, starting transfers between devices, along(): return lax.ppermute(array, 'grp', pairs)  21.3 us
    all_to_all x1, starting transfers between devices, per_device(): incoming = swap(outgoing, 'orb')  16.7 us
    all_to_all x1, blocking collectives, per_device(): boxes = swap(boxes, 'grp')  16 us
    all_to_all x1, blocking collectives, per_device(): terms = swap(terms, 'grp')  15.5 us
    pallas_call x1, Pallas kernels, pair_terms(): pl.pallas_call(functools.partial(solve_kernel, homes, share), out_shape=j...  5.65 us
    all_to_all x1, waiting for transfers between devices, per_device(): incoming = swap(outgoing, 'orb')  4.23 us
    pallas_call x4, Pallas kernels, rows_call(): pl.pallas_call(kernel, out_shape=out, in_specs=in_specs, out_specs=(VMEM,...  3.32 us
    pallas_call x1, Pallas kernels, plane_tables(): pl.pallas_call(plane_kernel, out_shape=jax.ShapeDtypeStruct((TABLES, PLAN...  3.1 us
  transfers between devices with their start and end apart: 7, of which 2 were waited for; matrix products, arithmetic and copies ran while one was open for 3% of the time, Pallas kernels for 5%

profile of v3, /device:TPU:1, one launch (start us, length us, event | category | flops | bytes accessed | tf_op | source)
XLA Modules:
  0.0 94.3 jit_solution(18231991859858572200)
XLA Ops:
  0.0 0.8 slice_bitcast_fusion
  0.8 0.1 select_reduce_fusion
  0.9 0.2 fusion.1
  1.1 0.1 reshape.153
  1.2 0.1 select_reduce_fusion.1
  1.3 0.1 reshape.150
  1.4 0.1 copy.8
  1.5 0.1 copy.10
  1.6 0.1 copy.9
  1.6 0.1 reshape.151.sent_ref
  1.8 0.1 reshape.152
  1.8 0.1 pad_add_fusion
  1.9 0.1 reshape.154.local_ref.target_ref
  2.0 0.1 pad_add_fusion.3.place_ref
  2.1 0.0 copy-start
  2.1 0.9 %copy-done = bf16[64,2,1024]{2,1,0:T(2,128)(2,1)S(1)} copy-done((bf16[64,2,1024]{2,1,0:T(2,128)(2,1)S(1)}, bf16[64,2,1024]{2,1,0:T(2,128)(2,1)}, u32[]{:S(2)}) %copy-start) | copy-done | bytes 262168
  3.0 1.6 %pick_rows.1 = (bf16[128,2,1024]{2,1,0:T(2,128)(2,1)}, bf16[24,2,1024]{2,1,0:T(2,128)(2,1)S(1)}, bf16[24,2,1024]{2,1,0:T(2,128)(2,1)S(1)}, bf16[24,2,1024]{2,1,0:T(2,128)(2,1)S(1)}, bf16[24,2,1024]{2,1,0:T(2,128)(2,1)S(1)}) custom-call(s32[2]{0:T(128)S(1)} %pad_add_fusion.3.place_ref, s32[128]{0:T(128)S(1)} %reshape.151.sent_ref, ...), custom_call_target="tpu_custom_call" | custom-call | tf_op jit(solution)/shard_map/pick_rows/pallas_call | solution.py:263
  4.6 16.7 %all-to-all-start = ((bf16[128,2,1024]{2,1,0:T(2,128)(2,1)}), bf16[128,2,1024]{2,1,0:T(2,128)(2,1)S(1)}, u32[]{:S(2)}, u32[]{:S(2)}) async-start(bf16[128,2,1024]{2,1,0:T(2,128)(2,1)} %get-tuple-element.29), calls=%async_computation | async-start | bytes 1048576 | tf_op jit(solution)/shard_map/all_to_all | solution.py:357
  21.3 3.1 %collective-permute-start = (bf16[24,2,1024]{2,1,0:T(2,128)(2,1)S(1)}, bf16[24,2,1024]{2,1,0:T(2,128)(2,1)S(1)}, u32[]{:S(2)}, u32[]{:S(2)}) collective-permute-start(bf16[24,2,1024]{2,1,0:T(2,128)(2,1)S(1)} %get-tuple-element.31), channel_id=1, source_target_pairs={{0,1},{1,2},{2,3},{3,0},{4,5},{5,6},{6,7},{7,4},{8,9},{9,10},{10,1... | collective-permute-start | bytes 294920 | tf_op jit(solution)/shard_map/ppermute | solution.py:279
  24.5 4.4 %collective-permute-start.1 = (bf16[24,2,1024]{2,1,0:T(2,128)(2,1)S(1)}, bf16[24,2,1024]{2,1,0:T(2,128)(2,1)S(1)}, u32[]{:S(2)}, u32[]{:S(2)}) collective-permute-start(bf16[24,2,1024]{2,1,0:T(2,128)(2,1)S(1)} %get-tuple-element.32), channel_id=1, source_target_pairs={{0,2},{1,3},{2,0},{3,1},{4,6},{5,7},{6,4},{7,5},{8,10},{9,11},{10,... | collective-permute-start | bytes 294920 | tf_op jit(solution)/shard_map/ppermute | solution.py:279
  28.8 3.1 %collective-permute-start.2 = (bf16[24,2,1024]{2,1,0:T(2,128)(2,1)S(1)}, bf16[24,2,1024]{2,1,0:T(2,128)(2,1)S(1)}, u32[]{:S(2)}, u32[]{:S(2)}) collective-permute-start(bf16[24,2,1024]{2,1,0:T(2,128)(2,1)S(1)} %get-tuple-element.33), channel_id=1, source_target_pairs={{0,3},{1,0},{2,1},{3,2},{4,7},{5,4},{6,5},{7,6},{8,11},{9,8},{10,9... | collective-permute-start | bytes 294920 | tf_op jit(solution)/shard_map/ppermute | solution.py:279
  32.0 0.1 dynamic_slice.15
  32.1 0.1 dynamic_slice.13
  32.1 0.1 copy.12
  32.2 0.1 add.174
  32.3 0.1 copy.11
  32.4 0.1 reshape.156
  32.5 0.1 dynamic_slice.14
  32.6 0.1 dynamic_slice.12
  32.7 0.1 pad_add_fusion.5
  32.8 0.1 pad_add_fusion.4
  32.9 0.1 reduce_sum.69
  32.9 0.1 fusion.28
  33.0 0.2 compare_reduce_fusion
  33.2 0.1 sine_multiply_fusion.sine_ref
  33.4 0.1 add_divide_fusion.green_hbm
  33.5 0.1 convert_subtract_fusion
  33.6 0.1 pad_add_fusion.1
  33.7 0.1 reshape.155.picks_ref
  33.7 0.1 copy.14
  33.8 0.1 select_n.118
  33.9 0.1 reshape.158.weight_ref
  34.0 0.0 collective-permute-done.refs_1_
  34.0 0.0 collective-permute-done.1.refs_2_
  34.0 0.5 collective-permute-done.2.refs_3_
  34.5 0.6 turn_rows.1
  35.1 3.2 %collective-permute-start.3 = (bf16[24,2,1024]{2,1,0:T(2,128)(2,1)S(1)}, bf16[24,2,1024]{2,1,0:T(2,128)(2,1)S(1)}, u32[]{:S(2)}, u32[]{:S(2)}) collective-permute-start(bf16[24,2,1024]{2,1,0:T(2,128)(2,1)S(1)} %get-tuple-element.35), channel_id=1, source_target_pairs={{0,4},{1,5},{2,6},{3,7},{4,8},{5,9},{6,10},{7,11},{8,12},{9,13},{1... | collective-permute-start | bytes 294920 | tf_op jit(solution)/shard_map/ppermute | solution.py:279
  38.3 4.5 %collective-permute-start.4 = (bf16[24,2,1024]{2,1,0:T(2,128)(2,1)S(1)}, bf16[24,2,1024]{2,1,0:T(2,128)(2,1)S(1)}, u32[]{:S(2)}, u32[]{:S(2)}) collective-permute-start(bf16[24,2,1024]{2,1,0:T(2,128)(2,1)S(1)} %get-tuple-element.36), channel_id=1, source_target_pairs={{0,8},{1,9},{2,10},{3,11},{4,12},{5,13},{6,14},{7,15},{8,0},{9,1},... | collective-permute-start | bytes 294920 | tf_op jit(solution)/shard_map/ppermute | solution.py:279
  42.8 3.0 %collective-permute-start.5 = (bf16[24,2,1024]{2,1,0:T(2,128)(2,1)S(1)}, bf16[24,2,1024]{2,1,0:T(2,128)(2,1)S(1)}, u32[]{:S(2)}, u32[]{:S(2)}) collective-permute-start(bf16[24,2,1024]{2,1,0:T(2,128)(2,1)S(1)} %get-tuple-element.37), channel_id=1, source_target_pairs={{0,12},{1,13},{2,14},{3,15},{4,0},{5,1},{6,2},{7,3},{8,4},{9,5},{1... | collective-permute-start | bytes 294920 | tf_op jit(solution)/shard_map/ppermute | solution.py:279
  45.8 0.9 multiply_reduce_fusion
  46.7 0.1 copy.13
  46.8 0.1 reshape.157.moves_ref
  46.9 3.1 %plane_tables.1.table_hbm = bf16[10,1024,1024]{2,1,0:T(8,128)(2,1)} custom-call(f32[32,32]{1,0:T(8,128)S(1)} %sine_multiply_fusion.sine_ref), custom_call_target="tpu_custom_call" | custom-call | tf_op jit(solution)/shard_map/plane_tables/pallas_call | solution.py:76
  50.0 0.0 collective-permute-done.3.refs_1_
  50.0 0.0 collective-permute-done.4.refs_2_
  50.0 0.0 collective-permute-done.5.refs_3_
  50.0 0.6 settle_rows.1.local_ref
  50.6 4.2 %all-to-all-done.incoming_ref = bf16[128,2,1024]{2,1,0:T(2,128)(2,1)S(1)} async-done(((bf16[128,2,1024]{2,1,0:T(2,128)(2,1)}), bf16[128,2,1024]{2,1,0:T(2,128)(2,1)S(1)}, u32[]{:S(2)}, u32[]{:S(2)}) %all-to-all-start) | async-done | bytes 524320 | tf_op jit(solution)/shard_map/all_to_all | solution.py:357
  54.9 0.6 pack_rows.1
  55.5 16.0 %all_to_all.15.boxes_ref = bf16[96,2,1024]{2,1,0:T(2,128)(2,1)S(1)} all-to-all(bf16[96,2,1024]{2,1,0:T(2,128)(2,1)S(1)} %pack_rows.1), channel_id=1, replica_groups=mesh['orb'=32,'grp'=16] {'grp'}, dimensions={0} | all-to-all | bytes 786432 | tf_op jit(solution)/shard_map/all_to_all | solution.py:432
  71.4 5.6 %pair_terms.1 = f32[96,2,1024]{2,1,0:T(2,128)S(1)} custom-call(s32[18]{0:T(128)S(1)} %reshape.157.moves_ref, bf16[96,2,1024]{2,1,0:T(2,128)(2,1)S(1)} %all_to_all.15.boxes_ref, bf16[96,2,1024]{2,1,0:T(2,128)(2,1)S(1)} %settle_rows.1.local_ref, f32[32,32]{1,0:T(8,128)S(1)} %sine_multiply_fusion.sine_ref, f32[32,1024]{1,0:T(8,128)S(1)} %add_divide_fusion.green_hbm, ...), custom_call_target="tpu_custom_call" | custom-call | tf_op jit(solution)/shard_map/pair_terms/pallas_call | solution.py:298
  77.1 15.5 %all_to_all.16.terms_ref = f32[96,2,1024]{2,1,0:T(2,128)S(1)} all-to-all(f32[96,2,1024]{2,1,0:T(2,128)S(1)} %pair_terms.1), channel_id=1, replica_groups=mesh['orb'=32,'grp'=16] {'grp'}, dimensions={0} | all-to-all | bytes 1572864 | tf_op jit(solution)/shard_map/all_to_all | solution.py:434
  92.6 1.8 %sum_rows.1 = f32[64,2,1024]{2,1,0:T(2,128)} custom-call(s32[96]{0:T(128)S(1)} %reshape.154.local_ref.target_ref, f32[96]{0:T(128)S(1)} %reshape.158.weight_ref, f32[96,2,1024]{2,1,0:T(2,128)S(1)} %all_to_all.16.terms_ref), custom_call_target="tpu_custom_call" | custom-call | tf_op jit(solution)/shard_map/sum_rows/pallas_call | solution.py:283
  (12 shorter events, 0.1 us)
Async XLA Ops:
  2.1 1.0 %copy-start = (bf16[64,2,1024]{2,1,0:T(2,128)(2,1)S(1)}, bf16[64,2,1024]{2,1,0:T(2,128)(2,1)}, u32[]{:S(2)}) copy-start(bf16[64,2,1024]{2,1,0:T(2,128)(2,1)} %orbitals_ref.1) | copy-start | bytes 786436
  4.6 50.3 %all-to-all-start = ((bf16[128,2,1024]{2,1,0:T(2,128)(2,1)}), bf16[128,2,1024]{2,1,0:T(2,128)(2,1)S(1)}, u32[]{:S(2)}, u32[]{:S(2)}) async-start(bf16[128,2,1024]{2,1,0:T(2,128)(2,1)} %get-tuple-element.29), calls=%async_computation | async-start | bytes 1048576 | tf_op jit(solution)/shard_map/all_to_all | solution.py:357
  21.3 12.7 %collective-permute-start = (bf16[24,2,1024]{2,1,0:T(2,128)(2,1)S(1)}, bf16[24,2,1024]{2,1,0:T(2,128)(2,1)S(1)}, u32[]{:S(2)}, u32[]{:S(2)}) collective-permute-start(bf16[24,2,1024]{2,1,0:T(2,128)(2,1)S(1)} %get-tuple-element.31), channel_id=1, source_target_pairs={{0,1},{1,2},{2,3},{3,0},{4,5},{5,6},{6,7},{7,4},{8,9},{9,10},{10,1... | collective-permute-start | bytes 294920 | tf_op jit(solution)/shard_map/ppermute | solution.py:279
  24.5 9.5 %collective-permute-start.1 = (bf16[24,2,1024]{2,1,0:T(2,128)(2,1)S(1)}, bf16[24,2,1024]{2,1,0:T(2,128)(2,1)S(1)}, u32[]{:S(2)}, u32[]{:S(2)}) collective-permute-start(bf16[24,2,1024]{2,1,0:T(2,128)(2,1)S(1)} %get-tuple-element.32), channel_id=1, source_target_pairs={{0,2},{1,3},{2,0},{3,1},{4,6},{5,7},{6,4},{7,5},{8,10},{9,11},{10,... | collective-permute-start | bytes 294920 | tf_op jit(solution)/shard_map/ppermute | solution.py:279
  28.8 5.7 %collective-permute-start.2 = (bf16[24,2,1024]{2,1,0:T(2,128)(2,1)S(1)}, bf16[24,2,1024]{2,1,0:T(2,128)(2,1)S(1)}, u32[]{:S(2)}, u32[]{:S(2)}) collective-permute-start(bf16[24,2,1024]{2,1,0:T(2,128)(2,1)S(1)} %get-tuple-element.33), channel_id=1, source_target_pairs={{0,3},{1,0},{2,1},{3,2},{4,7},{5,4},{6,5},{7,6},{8,11},{9,8},{10,9... | collective-permute-start | bytes 294920 | tf_op jit(solution)/shard_map/ppermute | solution.py:279
  35.1 14.9 %collective-permute-start.3 = (bf16[24,2,1024]{2,1,0:T(2,128)(2,1)S(1)}, bf16[24,2,1024]{2,1,0:T(2,128)(2,1)S(1)}, u32[]{:S(2)}, u32[]{:S(2)}) collective-permute-start(bf16[24,2,1024]{2,1,0:T(2,128)(2,1)S(1)} %get-tuple-element.35), channel_id=1, source_target_pairs={{0,4},{1,5},{2,6},{3,7},{4,8},{5,9},{6,10},{7,11},{8,12},{9,13},{1... | collective-permute-start | bytes 294920 | tf_op jit(solution)/shard_map/ppermute | solution.py:279
  38.3 11.7 %collective-permute-start.4 = (bf16[24,2,1024]{2,1,0:T(2,128)(2,1)S(1)}, bf16[24,2,1024]{2,1,0:T(2,128)(2,1)S(1)}, u32[]{:S(2)}, u32[]{:S(2)}) collective-permute-start(bf16[24,2,1024]{2,1,0:T(2,128)(2,1)S(1)} %get-tuple-element.36), channel_id=1, source_target_pairs={{0,8},{1,9},{2,10},{3,11},{4,12},{5,13},{6,14},{7,15},{8,0},{9,1},... | collective-permute-start | bytes 294920 | tf_op jit(solution)/shard_map/ppermute | solution.py:279
  42.8 7.2 %collective-permute-start.5 = (bf16[24,2,1024]{2,1,0:T(2,128)(2,1)S(1)}, bf16[24,2,1024]{2,1,0:T(2,128)(2,1)S(1)}, u32[]{:S(2)}, u32[]{:S(2)}) collective-permute-start(bf16[24,2,1024]{2,1,0:T(2,128)(2,1)S(1)} %get-tuple-element.37), channel_id=1, source_target_pairs={{0,12},{1,13},{2,14},{3,15},{4,0},{5,1},{6,2},{7,3},{8,4},{9,5},{1... | collective-permute-start | bytes 294920 | tf_op jit(solution)/shard_map/ppermute | solution.py:279

commit v4 on v3

--- a/solution.py
+++ b/solution.py
@@ -10,6 +10,8 @@
 
 BOX = 32
 PLANE = BOX * BOX
+HALF = PLANE // 2
+LANES = 128
 ORB_GRP = 64
 CAP = 2
 SCREEN = 0.25
@@ -22,16 +24,19 @@
     )
 
 
+def plane_modes(lanes):
+    odd, place = lanes >> 9, lanes & (HALF - 1)
+    y = place >> 4
+    return y, 2 * (place & 15) + ((y + odd) & 1)
+
+
 def green_rows():
-    levels = 2.0 - 2.0 * jnp.cos(
-        math.pi * (jnp.arange(BOX).astype(jnp.float32) + 1.0) / (BOX + 1.0)
-    )
-    lanes = jnp.arange(PLANE, dtype=jnp.int32)
-
     def level(index):
         return 2.0 - 2.0 * jnp.cos(math.pi * (index.astype(jnp.float32) + 1.0) / (BOX + 1.0))
 
-    return 1.0 / (levels[:, None] + (level(lanes // BOX) + level(lanes % BOX))[None, :] + SCREEN)
+    y, z = plane_modes(jnp.arange(PLANE, dtype=jnp.int32))
+    x = level(jnp.arange(BOX, dtype=jnp.int32))
+    return 1.0 / (x[:, None] + (level(y) + level(z))[None, :] + SCREEN)
 
 
 def halves(value):
@@ -43,14 +48,19 @@
     return jnp.dot(a, b, preferred_element_type=jnp.float32)
 
 
-TABLES = 10
+def dot_back(a, b):
+    return lax.dot_general(a, b, (((1,), (1,)), ((), ())), preferred_element_type=jnp.float32)
+
+
+TABLES = 40
 
 
 def plane_kernel(sine_ref, tables_hbm, table_ref, sems):
     lane = lax.broadcasted_iota(jnp.int32, (BOX, PLANE), 1)
     row = lax.broadcasted_iota(jnp.int32, (BOX, PLANE), 0)
-    by_y = jnp.where((lane >> 5) == row, 1.0, 0.0).astype(jnp.bfloat16)
-    by_z = jnp.where((lane & (BOX - 1)) == row, 1.0, 0.0).astype(jnp.bfloat16)
+    y, z = plane_modes(lane)
+    by_y = jnp.where(y == row, 1.0, 0.0).astype(jnp.bfloat16)
+    by_z = jnp.where(z == row, 1.0, 0.0).astype(jnp.bfloat16)
     parts = []
     rest = sine_ref[...]
     for _ in range(3):
@@ -59,12 +69,15 @@
         rest = rest - piece.astype(jnp.float32)
     cols_y = dot(parts[0], by_y) + dot(parts[1], by_y) + dot(parts[2], by_y)
     cols_z = dot(parts[0], by_z) + dot(parts[1], by_z) + dot(parts[2], by_z)
-    for m in range(BOX):
+    for m in range(BOX // 2):
         high, low = halves(cols_y[m : m + 1, :] * cols_z)
-        table_ref[0, m * BOX : (m + 1) * BOX, :] = high
-        table_ref[1, m * BOX : (m + 1) * BOX, :] = low
+        part = slice(m * BOX, (m + 1) * BOX)
+        for odd in range(2):
+            modes = slice(odd * HALF, (odd + 1) * HALF)
+            table_ref[2 * odd, part, :] = high[:, modes]
+            table_ref[2 * odd + 1, part, :] = low[:, modes]
     copies = [
-        pltpu.make_async_copy(table_ref.at[n], tables_hbm.at[n], sems.at[n]) for n in range(2)
+        pltpu.make_async_copy(table_ref.at[n], tables_hbm.at[n], sems.at[n]) for n in range(4)
     ]
     for copy in copies:
         copy.start()
@@ -75,12 +88,12 @@
 def plane_tables(sine):
     return pl.pallas_call(
         plane_kernel,
-        out_shape=jax.ShapeDtypeStruct((TABLES, PLANE, PLANE), jnp.bfloat16),
+        out_shape=jax.ShapeDtypeStruct((TABLES, HALF, HALF), jnp.bfloat16),
         in_specs=[VMEM],
         out_specs=HBM,
         scratch_shapes=[
-            pltpu.VMEM((2, PLANE, PLANE), jnp.bfloat16),
-            pltpu.SemaphoreType.DMA((2,)),
+            pltpu.VMEM((4, HALF, HALF), jnp.bfloat16),
+            pltpu.SemaphoreType.DMA((4,)),
         ],
         compiler_params=SOLVE_LIMIT,
         name="plane_tables",
@@ -91,15 +104,47 @@
 PAIR = 2
 
 
-def pick_kernel(each, place_ref, sent_ref, local_ref, orbitals_ref, sent_out, *local_outs):
-    for n in range(sent_out.shape[0]):
-        sent_out[n] = orbitals_ref[sent_ref[n]]
+def pick_kernel(lists_ref, orbitals_ref, sent_out, *refs):
+    local_outs, (columns, rows, picks_ref, own_ref, sems) = refs[:SIDE], refs[SIDE:]
+    groups, pair_count = lists_ref.shape[1:]
+    slots_each, rows_each = groups * CAP // SIDE**2, pair_count // SIDE**2
+    each = slots_each + rows_each
+    me = lax.axis_index("orb")
+    x = lax.axis_index("grp") & (SIDE - 1)
+    second = lists_ref[1].astype(jnp.float32)
+    own_first = lists_ref[0, pl.ds(me, 1), :].astype(jnp.float32)
+    own_slot = lists_ref[2, pl.ds(me, 1), :]
+    group = lax.broadcasted_iota(jnp.int32, (groups, pair_count), 0)
+    lane = lax.broadcasted_iota(jnp.int32, (groups, LANES), 1)
+    table = jnp.zeros((groups, LANES), jnp.float32)
+    for c in range(CAP):
+        asked = jnp.where(lists_ref[2] == me * CAP + c, second, 0.0)
+        named = jnp.where(own_slot == group * CAP + c, own_first, 0.0)
+        table = jnp.where(lane == c, jnp.sum(asked, axis=1, keepdims=True), table)
+        table = jnp.where(lane == CAP + c, jnp.sum(named, axis=1, keepdims=True), table)
+    columns[...] = table.astype(jnp.int32)
+    rows[...] = jnp.zeros_like(rows)
+    rows[0:1, 0:pair_count] = own_first.astype(jnp.int32)
+    copies = [
+        pltpu.make_async_copy(columns, picks_ref, sems.at[0]),
+        pltpu.make_async_copy(rows, own_ref, sems.at[1]),
+    ]
+    for copy in copies:
+        copy.start()
+    for copy in copies:
+        copy.wait()
+    for n in range(groups):
+        for c in range(2 * CAP):
+            sent_out[n * 2 * CAP + c] = orbitals_ref[picks_ref[n, c]]
     for step, out_ref in enumerate(local_outs):
-        side = (place_ref[1] + step) & (SIDE - 1)
-        for other in range(SIDE):
-            for q in range(each):
-                pick = local_ref[(other * SIDE + side) * each + q]
-                out_ref[other * each + q] = orbitals_ref[pick]
+        for y in range(SIDE):
+            side = y * SIDE + ((x + step) & (SIDE - 1))
+            for q in range(slots_each):
+                pick = picks_ref[side * (slots_each // CAP) + q // CAP, q % CAP]
+                out_ref[y * each + q] = orbitals_ref[pick]
+            for q in range(rows_each):
+                pick = own_ref[0, side * rows_each + q]
+                out_ref[y * each + slots_each + q] = orbitals_ref[pick]
 
 
 def turn_kernel(each, place_ref, *refs):
@@ -181,11 +226,8 @@
     depth = boxes_ref.shape[1]
     sides = BOX // depth
     copies = [
-        pltpu.make_async_copy(source, into, sems.at[n])
-        for n, (source, into) in enumerate(
-            ((table_hbm.at[0], table_ref.at[0]), (table_hbm.at[1], table_ref.at[1]), (green_hbm, green_ref))
-        )
-    ]
+        pltpu.make_async_copy(table_hbm.at[n], table_ref.at[n], sems.at[n]) for n in range(4)
+    ] + [pltpu.make_async_copy(green_hbm, green_ref, sems.at[4])]
     for copy in copies:
         copy.start()
     for s in range(sides):
@@ -206,10 +248,31 @@
         high, low = halves(value)
         return dot(three, jnp.concatenate([high, low, high], 0))
 
-    def along_plane(value):
-        high, low = halves(value)
-        both = dot(jnp.concatenate([high, low], 0), table_ref[0])
-        return both[:rows] + both[rows:] + dot(high, table_ref[1])
+    def mirrored(value):
+        back = LANES - 1 - lax.broadcasted_iota(jnp.int32, (value.shape[0], LANES), 1)
+        blocks = [value[:, n : n + LANES] for n in range(0, HALF, LANES)]
+        return jnp.concatenate(
+            [jnp.take_along_axis(block, back, axis=1) for block in reversed(blocks)], 1
+        )
+
+    def to_modes(value):
+        near, far = value[:, :HALF], mirrored(value[:, HALF:])
+        modes = []
+        for n, part in ((0, near + far), (2, near - far)):
+            high, low = halves(part)
+            copies[n].wait()
+            both = dot(jnp.concatenate([high, low], 0), table_ref[n])
+            copies[n + 1].wait()
+            modes.append(both[:rows] + both[rows:] + dot(high, table_ref[n + 1]))
+        return jnp.concatenate(modes, 1)
+
+    def to_cells(modes):
+        even, odd = [], []
+        for n, part, into in ((0, modes[:, :HALF], even), (2, modes[:, HALF:], odd)):
+            high, low = halves(part)
+            both = dot_back(jnp.concatenate([high, low], 0), table_ref[n])
+            into.append(both[:rows] + both[rows:] + dot_back(high, table_ref[n + 1]))
+        return jnp.concatenate([even[0] + odd[0], mirrored(even[0] - odd[0])], 1)
 
     charges = []
     for at in range(0, share, PAIR):
@@ -223,13 +286,9 @@
         if at < homes:
             second[part, :] = shifted
         charges.append(along_x(first[part, :] * shifted))
-    copies[0].wait()
-    high, low = halves(jnp.concatenate(charges, 0))
-    both = dot(jnp.concatenate([high, low], 0), table_ref[0])
-    copies[1].wait()
-    modes = both[:rows] + both[rows:] + dot(high, table_ref[1])
-    copies[2].wait()
-    held[...] = along_plane(modes * jnp.concatenate([green_ref[...]] * share, 0))
+    modes = to_modes(jnp.concatenate(charges, 0))
+    copies[4].wait()
+    held[...] = to_cells(modes * jnp.concatenate([green_ref[...]] * share, 0))
     for at in range(0, share, PAIR):
         part = slice(at * BOX, (at + PAIR) * BOX)
         potential = along_x(held[part, :])
@@ -255,17 +314,19 @@
 SMEM = pl.BlockSpec(memory_space=pltpu.SMEM)
 HBM = pl.BlockSpec(memory_space=pltpu.HBM)
 ROWS_LIMIT = pltpu.CompilerParams(vmem_limit_bytes=20 << 20)
+PICK_LIMIT = pltpu.CompilerParams(vmem_limit_bytes=66_900_000)
 SOLVE_LIMIT = pltpu.CompilerParams(vmem_limit_bytes=46 << 20)
 
 
-def rows_call(kernel, name, counts, in_specs, box, *args):
+def rows_call(kernel, name, counts, in_specs, box, *args, scratch=(), limit=ROWS_LIMIT):
     out = tuple(jax.ShapeDtypeStruct((n, *box.shape[1:]), box.dtype) for n in counts)
     return pl.pallas_call(
         kernel,
         out_shape=out,
         in_specs=in_specs,
         out_specs=(VMEM,) * len(out),
-        compiler_params=ROWS_LIMIT,
+        scratch_shapes=scratch,
+        compiler_params=limit,
         name=name,
     )(*args)
 
@@ -294,7 +355,7 @@
 def pair_terms(homes, boxes, local, moves, table, green, sine):
     share = moves.shape[0] // 3
     cube = pltpu.VMEM((share * BOX, PLANE), jnp.float32)
-    halves_type = pltpu.VMEM((2, PLANE, PLANE), jnp.bfloat16)
+    halves_type = pltpu.VMEM((4, HALF, HALF), jnp.bfloat16)
     return pl.pallas_call(
         functools.partial(solve_kernel, homes, share),
         out_shape=jax.ShapeDtypeStruct(boxes.shape, jnp.float32),
@@ -306,7 +367,7 @@
             cube,
             pltpu.VMEM((BOX, PLANE), jnp.float32),
             halves_type,
-            pltpu.SemaphoreType.DMA((3,)),
+            pltpu.SemaphoreType.DMA((5,)),
         ],
         compiler_params=SOLVE_LIMIT,
         name="pair_terms",
@@ -325,37 +386,29 @@
     slots_each = slot_count // layers
     swap = functools.partial(lax.all_to_all, split_axis=0, concat_axis=0, tiled=True)
 
-    pair_list = lax.optimization_barrier(tuple(pair_list[:, :, n] for n in range(3)))
-    is_me = jnp.arange(groups, dtype=jnp.int32)[:, None] == me
-    first_local, second_local, slot = (
-        jnp.sum(jnp.where(is_me, plane_of, 0), axis=0) for plane_of in pair_list
-    )
-    wanted = me * CAP + jnp.arange(CAP, dtype=jnp.int32)
-    asked = pair_list[2][:, None, :] == wanted[None, :, None]
-    home_second = jnp.sum(jnp.where(asked, pair_list[1][:, None, :], 0), axis=2)
-    slot_ids = jnp.arange(slot_count, dtype=jnp.int32)
-    named = slot[None, :] == slot_ids[:, None]
-    sent_first = jnp.sum(jnp.where(named, first_local[None, :], 0), axis=1).reshape(groups, CAP)
-    outgoing = jnp.concatenate([home_second, sent_first], axis=1).reshape(2 * slot_count)
-    local = jnp.concatenate(
-        [home_second.reshape(layers, slots_each), first_local.reshape(layers, rows_each)], axis=1
-    ).reshape(-1)
     each = rows_each + slots_each
     side_rows = SIDE * each
-    place = jnp.stack([region // SIDE, region % SIDE])
+    lists = jnp.transpose(pair_list, (2, 0, 1))
     outgoing, *local_rows = rows_call(
-        functools.partial(pick_kernel, each),
+        pick_kernel,
         "pick_rows",
         (2 * slot_count,) + (side_rows,) * SIDE,
-        [SMEM, SMEM, SMEM, VMEM],
+        [VMEM, VMEM],
         orbitals,
-        place,
-        outgoing,
-        local,
+        lists,
         orbitals,
+        scratch=[
+            pltpu.VMEM((groups, LANES), jnp.int32),
+            pltpu.VMEM((8, LANES), jnp.int32),
+            pltpu.SMEM((groups, LANES), jnp.int32),
+            pltpu.SMEM((8, LANES), jnp.int32),
+            pltpu.SemaphoreType.DMA((2,)),
+        ],
+        limit=PICK_LIMIT,
     )
     incoming = swap(outgoing, "orb")
 
+    place = jnp.stack([region // SIDE, region % SIDE])
     came = [local_rows[0]] + [along(local_rows[n], n, 1) for n in range(1, SIDE)]
     turned = rows_call(
         functools.partial(turn_kernel, each),
@@ -377,9 +430,20 @@
         *(along(turned[n], n, 0) for n in range(1, SIDE)),
     )
 
-    home_second = home_second.reshape(slot_count)
+    first_of, second_of, slot_of = lax.optimization_barrier(tuple(lists[n] for n in range(3)))
+    is_me = jnp.arange(groups, dtype=jnp.int32)[:, None] == me
+    first_local, second_local, slot = (
+        jnp.sum(jnp.where(is_me, values, 0), axis=0) for values in (first_of, second_of, slot_of)
+    )
+    slot_ids = jnp.arange(slot_count, dtype=jnp.int32)
+    wanted = me * CAP + jnp.arange(CAP, dtype=jnp.int32)
+    asked = slot_of[:, None, :] == wanted[None, :, None]
+    home_second = jnp.sum(jnp.where(asked, second_of[:, None, :], 0), axis=2).reshape(slot_count)
+    local = jnp.concatenate(
+        [home_second.reshape(layers, slots_each), first_local.reshape(layers, rows_each)], axis=1
+    ).reshape(-1)
     home_valid = jnp.any(asked, axis=2).reshape(slot_count)
-    home_first = jnp.sum(jnp.where(asked, pair_list[0][:, None, :], 0), axis=2).reshape(slot_count)
+    home_first = jnp.sum(jnp.where(asked, first_of[:, None, :], 0), axis=2).reshape(slot_count)
     from_rows = (slot // CAP * (2 * CAP) + slot % CAP).reshape(layers, rows_each)
     from_slots = (slot_ids // CAP * (2 * CAP) + CAP + slot_ids % CAP).reshape(layers, slots_each)
     from_incoming = jnp.concatenate([from_rows, from_slots], axis=1).reshape(-1)

time: 95.3 us -> 93 us (0.976)
  waiting for transfers between devices: 4.71 us -> 3.32 us
    pallas_call x4, Pallas kernels: 3.32 us -> 4.84 us  [rows_call(): pl.pallas_call(kernel, out_shape=out, in_specs=in_specs, out_specs=(VMEM,...]
    pallas_call x1, Pallas kernels: 3.1 us -> 2.02 us  [plane_tables(): pl.pallas_call(plane_kernel, out_shape=jax.ShapeDtypeStruct((TABLES, HALF...]
  transfers between devices with their start and end apart: 7 -> 7, of which waited for: 2 -> 1; matrix products, arithmetic and copies ran while one was open for 3% -> 5% of each run, Pallas kernels for 5% -> 3%
where the time goes in v4:
time: 93 us; the launch traced here: 92 us
  starting transfers between devices  38 us (41%)
  blocking collectives  31.4 us (34%)
  Pallas kernels  13.5 us (15%)
  waiting for transfers between devices  3.32 us (4%)
  local copies, waits for them, and re-layouts  3.28 us (4%)
  other arithmetic  2.29 us (2%)
    ppermute x6, starting transfers between devices, along(): return lax.ppermute(array, 'grp', pairs)  21.2 us
    all_to_all x1, starting transfers between devices, per_device(): incoming = swap(outgoing, 'orb')  16.7 us
    all_to_all x1, blocking collectives, per_device(): boxes = swap(boxes, 'grp')  16 us
    all_to_all x1, blocking collectives, per_device(): terms = swap(terms, 'grp')  15.5 us
    pallas_call x4, Pallas kernels, rows_call(): pl.pallas_call(kernel, out_shape=out, in_specs=in_specs, out_specs=(VMEM,...  4.84 us
    pallas_call x1, Pallas kernels, pair_terms(): pl.pallas_call(functools.partial(solve_kernel, homes, share), out_shape=j...  4.84 us
    all_to_all x1, waiting for transfers between devices, per_device(): incoming = swap(outgoing, 'orb')  3.3 us
    pallas_call x1, Pallas kernels, plane_tables(): pl.pallas_call(plane_kernel, out_shape=jax.ShapeDtypeStruct((TABLES, HALF...  2.02 us
  transfers between devices with their start and end apart: 7, of which 1 were waited for; matrix products, arithmetic and copies ran while one was open for 5% of the time, Pallas kernels for 3%

profile of v4, /device:TPU:1, one launch (start us, length us, event | category | flops | bytes accessed | tf_op | source)
XLA Modules:
  0.0 92.0 jit_solution(8880308689282108549)
XLA Ops:
  0.0 3.1 %pick_rows.1 = (bf16[128,2,1024]{2,1,0:T(2,128)(2,1)}, bf16[24,2,1024]{2,1,0:T(2,128)(2,1)}, bf16[24,2,1024]{2,1,0:T(2,128)(2,1)}, bf16[24,2,1024]{2,1,0:T(2,128)(2,1)}, bf16[24,2,1024]{2,1,0:T(2,128)(2,1)}) custom-call(s32[3,32,32]{2,1,0:T(8,128)} %bitcast.10, bf16[64,2,1024]{2,1,0:T(2,128)(2,1)} %orbitals_ref.1), custom_call_target="tpu_custom_call" | custom-call | tf_op jit(solution)/shard_map/pick_rows/pallas_call | solution.py:323
  3.1 16.7 %all-to-all-start = ((bf16[128,2,1024]{2,1,0:T(2,128)(2,1)}), bf16[128,2,1024]{2,1,0:T(2,128)(2,1)S(1)}, u32[]{:S(2)}, u32[]{:S(2)}) async-start(bf16[128,2,1024]{2,1,0:T(2,128)(2,1)} %get-tuple-element.26), calls=%async_computation | async-start | bytes 1048576 | tf_op jit(solution)/shard_map/all_to_all | solution.py:409
  19.8 3.1 %collective-permute-start = (bf16[24,2,1024]{2,1,0:T(2,128)(2,1)}, bf16[24,2,1024]{2,1,0:T(2,128)(2,1)S(1)}, u32[]{:S(2)}, u32[]{:S(2)}) collective-permute-start(bf16[24,2,1024]{2,1,0:T(2,128)(2,1)} %get-tuple-element.29), channel_id=1, source_target_pairs={{0,1},{1,2},{2,3},{3,0},{4,5},{5,6},{6,7},{7,4},{8,9},{9,10},{10,1... | collective-permute-start | bytes 294920 | tf_op jit(solution)/shard_map/ppermute | solution.py:340
  23.0 4.4 %collective-permute-start.1 = (bf16[24,2,1024]{2,1,0:T(2,128)(2,1)}, bf16[24,2,1024]{2,1,0:T(2,128)(2,1)S(1)}, u32[]{:S(2)}, u32[]{:S(2)}) collective-permute-start(bf16[24,2,1024]{2,1,0:T(2,128)(2,1)} %get-tuple-element.30), channel_id=1, source_target_pairs={{0,2},{1,3},{2,0},{3,1},{4,6},{5,7},{6,4},{7,5},{8,10},{9,11},{10,... | collective-permute-start | bytes 294920 | tf_op jit(solution)/shard_map/ppermute | solution.py:340
  27.3 3.1 %collective-permute-start.2 = (bf16[24,2,1024]{2,1,0:T(2,128)(2,1)}, bf16[24,2,1024]{2,1,0:T(2,128)(2,1)S(1)}, u32[]{:S(2)}, u32[]{:S(2)}) collective-permute-start(bf16[24,2,1024]{2,1,0:T(2,128)(2,1)} %get-tuple-element.31), channel_id=1, source_target_pairs={{0,3},{1,0},{2,1},{3,2},{4,7},{5,4},{6,5},{7,6},{8,11},{9,8},{10,9... | collective-permute-start | bytes 294920 | tf_op jit(solution)/shard_map/ppermute | solution.py:340
  30.4 0.8 slice_bitcast_fusion
  31.2 0.1 select_reduce_fusion.1
  31.3 0.2 fusion
  31.5 0.1 copy.7
  31.6 0.1 reshape.134
  31.7 0.1 reduce_sum.57
  31.8 0.1 reshape_reshape.3
  31.9 0.1 copy.4
  32.0 0.1 reshape.132
  32.1 0.1 pad_add_fusion
  32.2 0.1 pad_add_fusion.1
  32.3 0.1 dynamic_slice.15
  32.3 0.1 dynamic_slice.13
  32.4 0.1 reshape.131.picks_ref
  32.5 0.1 reshape.135.target_ref
  32.6 0.1 copy.5
  32.7 0.1 add.173
  32.8 0.1 dynamic_slice.14
  32.9 0.1 dynamic_slice.12
  33.0 0.2 compare_reduce_fusion
  33.1 0.1 copy.8
  33.2 0.1 select_n.92
  33.3 0.1 reshape.136.weight_ref
  33.5 0.1 pad_add_fusion.4
  33.5 0.1 pad_add_fusion.3
  33.6 0.1 fusion.25
  33.7 0.1 sine_multiply_fusion.sine_ref
  33.8 0.1 add_divide_fusion.green_hbm
  33.9 0.1 convert_subtract_fusion
  34.0 0.1 pad_add_fusion.2.place_ref
  34.1 0.0 collective-permute-done.refs_1_
  34.1 0.0 collective-permute-done.1.refs_2_
  34.1 0.0 collective-permute-done.2.refs_3_
  34.1 0.0 copy-start
  34.1 0.9 copy-done
  35.0 0.6 turn_rows.1
  35.6 3.2 %collective-permute-start.3 = (bf16[24,2,1024]{2,1,0:T(2,128)(2,1)S(1)}, bf16[24,2,1024]{2,1,0:T(2,128)(2,1)S(1)}, u32[]{:S(2)}, u32[]{:S(2)}) collective-permute-start(bf16[24,2,1024]{2,1,0:T(2,128)(2,1)S(1)} %get-tuple-element.33), channel_id=1, source_target_pairs={{0,4},{1,5},{2,6},{3,7},{4,8},{5,9},{6,10},{7,11},{8,12},{9,13},{1... | collective-permute-start | bytes 294920 | tf_op jit(solution)/shard_map/ppermute | solution.py:340
  38.8 4.5 %collective-permute-start.4 = (bf16[24,2,1024]{2,1,0:T(2,128)(2,1)S(1)}, bf16[24,2,1024]{2,1,0:T(2,128)(2,1)S(1)}, u32[]{:S(2)}, u32[]{:S(2)}) collective-permute-start(bf16[24,2,1024]{2,1,0:T(2,128)(2,1)S(1)} %get-tuple-element.34), channel_id=1, source_target_pairs={{0,8},{1,9},{2,10},{3,11},{4,12},{5,13},{6,14},{7,15},{8,0},{9,1},... | collective-permute-start | bytes 294920 | tf_op jit(solution)/shard_map/ppermute | solution.py:340
  43.3 3.0 %collective-permute-start.5 = (bf16[24,2,1024]{2,1,0:T(2,128)(2,1)S(1)}, bf16[24,2,1024]{2,1,0:T(2,128)(2,1)S(1)}, u32[]{:S(2)}, u32[]{:S(2)}) collective-permute-start(bf16[24,2,1024]{2,1,0:T(2,128)(2,1)S(1)} %get-tuple-element.35), channel_id=1, source_target_pairs={{0,12},{1,13},{2,14},{3,15},{4,0},{5,1},{6,2},{7,3},{8,4},{9,5},{1... | collective-permute-start | bytes 294920 | tf_op jit(solution)/shard_map/ppermute | solution.py:340
  46.3 0.9 %multiply_reduce_fusion = s32[6,3]{0,1:T(4,128)S(1)} fusion(s32[3,2048]{1,0:T(4,128)} %bitcast.12, s32[6,2048]{1,0:T(8,128)S(1)} %convert_subtract_fusion), kind=kLoop, calls=%fused_computation | loop fusion | flops 73710 | bytes 73800 | tf_op jit(solution)/shard_map/reduce_sum | solution.py:470
  47.2 0.1 copy.6
  47.3 0.1 reshape.133.moves_ref
  47.4 2.0 %plane_tables.1.table_hbm = bf16[40,512,512]{2,1,0:T(8,128)(2,1)} custom-call(f32[32,32]{1,0:T(8,128)S(1)} %sine_multiply_fusion.sine_ref), custom_call_target="tpu_custom_call" | custom-call | tf_op jit(solution)/shard_map/plane_tables/pallas_call | solution.py:89
  49.4 0.0 collective-permute-done.3.refs_1_
  49.5 0.0 collective-permute-done.4.refs_2_
  49.5 0.0 collective-permute-done.5.refs_3_
  49.5 0.6 settle_rows.1.local_ref
  50.1 3.3 %all-to-all-done.incoming_ref = bf16[128,2,1024]{2,1,0:T(2,128)(2,1)S(1)} async-done(((bf16[128,2,1024]{2,1,0:T(2,128)(2,1)}), bf16[128,2,1024]{2,1,0:T(2,128)(2,1)S(1)}, u32[]{:S(2)}, u32[]{:S(2)}) %all-to-all-start) | async-done | bytes 524320 | tf_op jit(solution)/shard_map/all_to_all | solution.py:409
  53.4 0.6 pack_rows.1
  54.0 16.0 %all_to_all.15.boxes_ref = bf16[96,2,1024]{2,1,0:T(2,128)(2,1)S(1)} all-to-all(bf16[96,2,1024]{2,1,0:T(2,128)(2,1)S(1)} %pack_rows.1), channel_id=1, replica_groups=mesh['orb'=32,'grp'=16] {'grp'}, dimensions={0} | all-to-all | bytes 786432 | tf_op jit(solution)/shard_map/all_to_all | solution.py:496
  69.9 4.8 %pair_terms.1 = f32[96,2,1024]{2,1,0:T(2,128)S(1)} custom-call(s32[18]{0:T(128)S(1)} %reshape.133.moves_ref, bf16[96,2,1024]{2,1,0:T(2,128)(2,1)S(1)} %all_to_all.15.boxes_ref, bf16[96,2,1024]{2,1,0:T(2,128)(2,1)S(1)} %settle_rows.1.local_ref, f32[32,32]{1,0:T(8,128)S(1)} %sine_multiply_fusion.sine_ref, f32[32,1024]{1,0:T(8,128)S(1)} %add_divide_fusion.green_hbm, ...), custom_call_target="tpu_custom_call" | custom-call | tf_op jit(solution)/shard_map/pair_terms/pallas_call | solution.py:359
  74.8 15.5 %all_to_all.16.terms_ref = f32[96,2,1024]{2,1,0:T(2,128)S(1)} all-to-all(f32[96,2,1024]{2,1,0:T(2,128)S(1)} %pair_terms.1), channel_id=1, replica_groups=mesh['orb'=32,'grp'=16] {'grp'}, dimensions={0} | all-to-all | bytes 1572864 | tf_op jit(solution)/shard_map/all_to_all | solution.py:498
  90.2 1.8 %sum_rows.1 = f32[64,2,1024]{2,1,0:T(2,128)} custom-call(s32[96]{0:T(128)S(1)} %reshape.135.target_ref, f32[96]{0:T(128)S(1)} %reshape.136.weight_ref, f32[96,2,1024]{2,1,0:T(2,128)S(1)} %all_to_all.16.terms_ref), custom_call_target="tpu_custom_call" | custom-call | tf_op jit(solution)/shard_map/sum_rows/pallas_call | solution.py:344
  (11 shorter events, 0.1 us)
Async XLA Ops:
  3.1 50.3 %all-to-all-start = ((bf16[128,2,1024]{2,1,0:T(2,128)(2,1)}), bf16[128,2,1024]{2,1,0:T(2,128)(2,1)S(1)}, u32[]{:S(2)}, u32[]{:S(2)}) async-start(bf16[128,2,1024]{2,1,0:T(2,128)(2,1)} %get-tuple-element.26), calls=%async_computation | async-start | bytes 1048576 | tf_op jit(solution)/shard_map/all_to_all | solution.py:409
  19.8 14.3 %collective-permute-start = (bf16[24,2,1024]{2,1,0:T(2,128)(2,1)}, bf16[24,2,1024]{2,1,0:T(2,128)(2,1)S(1)}, u32[]{:S(2)}, u32[]{:S(2)}) collective-permute-start(bf16[24,2,1024]{2,1,0:T(2,128)(2,1)} %get-tuple-element.29), channel_id=1, source_target_pairs={{0,1},{1,2},{2,3},{3,0},{4,5},{5,6},{6,7},{7,4},{8,9},{9,10},{10,1... | collective-permute-start | bytes 294920 | tf_op jit(solution)/shard_map/ppermute | solution.py:340
  23.0 11.1 %collective-permute-start.1 = (bf16[24,2,1024]{2,1,0:T(2,128)(2,1)}, bf16[24,2,1024]{2,1,0:T(2,128)(2,1)S(1)}, u32[]{:S(2)}, u32[]{:S(2)}) collective-permute-start(bf16[24,2,1024]{2,1,0:T(2,128)(2,1)} %get-tuple-element.30), channel_id=1, source_target_pairs={{0,2},{1,3},{2,0},{3,1},{4,6},{5,7},{6,4},{7,5},{8,10},{9,11},{10,... | collective-permute-start | bytes 294920 | tf_op jit(solution)/shard_map/ppermute | solution.py:340
  27.3 6.8 %collective-permute-start.2 = (bf16[24,2,1024]{2,1,0:T(2,128)(2,1)}, bf16[24,2,1024]{2,1,0:T(2,128)(2,1)S(1)}, u32[]{:S(2)}, u32[]{:S(2)}) collective-permute-start(bf16[24,2,1024]{2,1,0:T(2,128)(2,1)} %get-tuple-element.31), channel_id=1, source_target_pairs={{0,3},{1,0},{2,1},{3,2},{4,7},{5,4},{6,5},{7,6},{8,11},{9,8},{10,9... | collective-permute-start | bytes 294920 | tf_op jit(solution)/shard_map/ppermute | solution.py:340
  34.1 0.9 copy-start
  35.6 13.9 %collective-permute-start.3 = (bf16[24,2,1024]{2,1,0:T(2,128)(2,1)S(1)}, bf16[24,2,1024]{2,1,0:T(2,128)(2,1)S(1)}, u32[]{:S(2)}, u32[]{:S(2)}) collective-permute-start(bf16[24,2,1024]{2,1,0:T(2,128)(2,1)S(1)} %get-tuple-element.33), channel_id=1, source_target_pairs={{0,4},{1,5},{2,6},{3,7},{4,8},{5,9},{6,10},{7,11},{8,12},{9,13},{1... | collective-permute-start | bytes 294920 | tf_op jit(solution)/shard_map/ppermute | solution.py:340
  38.8 10.7 %collective-permute-start.4 = (bf16[24,2,1024]{2,1,0:T(2,128)(2,1)S(1)}, bf16[24,2,1024]{2,1,0:T(2,128)(2,1)S(1)}, u32[]{:S(2)}, u32[]{:S(2)}) collective-permute-start(bf16[24,2,1024]{2,1,0:T(2,128)(2,1)S(1)} %get-tuple-element.34), channel_id=1, source_target_pairs={{0,8},{1,9},{2,10},{3,11},{4,12},{5,13},{6,14},{7,15},{8,0},{9,1},... | collective-permute-start | bytes 294920 | tf_op jit(solution)/shard_map/ppermute | solution.py:340
  43.3 6.1 %collective-permute-start.5 = (bf16[24,2,1024]{2,1,0:T(2,128)(2,1)S(1)}, bf16[24,2,1024]{2,1,0:T(2,128)(2,1)S(1)}, u32[]{:S(2)}, u32[]{:S(2)}) collective-permute-start(bf16[24,2,1024]{2,1,0:T(2,128)(2,1)S(1)} %get-tuple-element.35), channel_id=1, source_target_pairs={{0,12},{1,13},{2,14},{3,15},{4,0},{5,1},{6,2},{7,3},{8,4},{9,5},{1... | collective-permute-start | bytes 294920 | tf_op jit(solution)/shard_map/ppermute | solution.py:340

commit v5 on v4

--- a/solution.py
+++ b/solution.py
@@ -12,6 +12,8 @@
 PLANE = BOX * BOX
 HALF = PLANE // 2
 LANES = 128
+SUBLANES = 8
+TOP_EXP = 14.0
 ORB_GRP = 64
 CAP = 2
 SCREEN = 0.25
@@ -171,15 +173,29 @@
         out_ref[n] = incoming_ref[picks_ref[n]]
 
 
-def sum_kernel(target_ref, weight_ref, terms_ref, out_ref, *sums):
-    sums = (out_ref, *sums)
+def sum_kernel(share, depth, target_ref, terms_ref, out_ref, *sums):
     for held in sums:
         held[...] = jnp.zeros_like(held)
-    for n in range(terms_ref.shape[0]):
-        at = target_ref[n]
-        held = sums[n % len(sums)]
-        held[at] = held[at] + weight_ref[n] * terms_ref[n]
-    out_ref[...] = sum(held[...] for held in sums)
+    chunks = PLANE // LANES
+    block = depth * chunks
+    each_x = terms_ref.shape[1] // depth
+    for s in range(terms_ref.shape[0]):
+        gains = jnp.exp2(-terms_ref[s, share * chunks : share * chunks + 1, :])
+        for k in range(share):
+            n = s * share + k
+            held = sums[n % len(sums)]
+            at = pl.ds(pl.multiple_of(target_ref[n] * block, block), block)
+            term = [
+                terms_ref[s, x * each_x + k * chunks : x * each_x + (k + 1) * chunks, :]
+                for x in range(depth)
+            ]
+            held[at, :] = held[at, :] + jnp.concatenate(term, 0) * gains[:, k : k + 1]
+    total = sums[0]
+    total[...] = sum(held[...] for held in sums)
+    for n in range(out_ref.shape[0]):
+        for c in range(chunks):
+            cells = pl.ds(n * block + c, depth, stride=chunks)
+            out_ref[n, :, c * LANES : (c + 1) * LANES] = total[cells, :]
 
 
 def same_pair():
@@ -192,7 +208,7 @@
     row, col, same = same_pair()
     step = jnp.zeros(row.shape, jnp.int32)
     for k in range(PAIR):
-        step = jnp.where((row >> 5) == k, moves_ref[3 * (at + k)], step)
+        step = jnp.where((row >> 5) == k, moves_ref[at + k, 0], step)
     hit = (row == col + step) if back else (col == row + step)
     return jnp.where(same & hit, 1.0, 0.0).astype(jnp.bfloat16)
 
@@ -208,16 +224,18 @@
 def solve_kernel(
     homes,
     share,
-    moves_ref,
     boxes_ref,
     local_ref,
-    sine_ref,
+    moves_hbm,
+    sine_hbm,
     green_hbm,
     table_hbm,
     out_ref,
     first,
     second,
     held,
+    moves_ref,
+    sine_ref,
     green_ref,
     table_ref,
     sems,
@@ -227,9 +245,14 @@
     sides = BOX // depth
     copies = [
         pltpu.make_async_copy(table_hbm.at[n], table_ref.at[n], sems.at[n]) for n in range(4)
-    ] + [pltpu.make_async_copy(green_hbm, green_ref, sems.at[4])]
-    for copy in copies:
-        copy.start()
+    ] + [
+        pltpu.make_async_copy(source, into, sems.at[4 + n])
+        for n, (source, into) in enumerate(
+            ((green_hbm, green_ref), (moves_hbm, moves_ref), (sine_hbm, sine_ref))
+        )
+    ]
+    for n in (5, 6, 0, 1, 2, 3, 4):
+        copies[n].start()
     for s in range(sides):
         for k in range(share):
             at = k * BOX + s * depth
@@ -239,6 +262,8 @@
             other = first if k < homes else second
             other[at : at + depth, :] = local_ref[s * share + k].astype(jnp.float32)
 
+    copies[5].wait()
+    copies[6].wait()
     _, _, same = same_pair()
     wide = jnp.concatenate([jnp.concatenate([sine_ref[...]] * PAIR, 1)] * PAIR, 0)
     sine_high, sine_low = halves(jnp.where(same, wide, 0.0))
@@ -277,7 +302,7 @@
     charges = []
     for at in range(0, share, PAIR):
         turned = [
-            moved(second[k * BOX : (k + 1) * BOX, :], moves_ref[3 * k + 1], moves_ref[3 * k + 2])
+            moved(second[k * BOX : (k + 1) * BOX, :], moves_ref[k, 1], moves_ref[k, 2])
             for k in range(at, at + PAIR)
         ]
         ahead = steps_along_x(moves_ref, at, False)
@@ -301,13 +326,27 @@
             for k in range(PAIR):
                 held[(at + k) * BOX : (at + k + 1) * BOX, :] = moved(
                     upright[k * BOX : (k + 1) * BOX],
-                    -moves_ref[3 * (at + k) + 1],
-                    -moves_ref[3 * (at + k) + 2],
+                    -moves_ref[at + k, 1],
+                    -moves_ref[at + k, 2],
                 )
-    for s in range(sides):
-        for k in range(share):
-            at = k * BOX + s * depth
-            out_ref[s * share + k] = held[at : at + depth, :]
+    each_x = out_ref.shape[0] // BOX
+    lane = lax.broadcasted_iota(jnp.int32, (SUBLANES, LANES), 1)
+    note = jnp.zeros((SUBLANES, LANES), jnp.float32)
+    for k in range(share):
+        value = held[k * BOX : (k + 1) * BOX, :]
+        peak = jnp.max(jnp.abs(value), axis=(0, 1), keepdims=True)
+        power = jnp.floor(TOP_EXP - jnp.log2(jnp.maximum(peak, 1e-30)))
+        note = jnp.where(lane == k, power, note)
+        value = value * jnp.exp2(power)
+        for x in range(0, BOX, SUBLANES):
+            for n in range(PLANE // LANES):
+                row = x * each_x + k * (PLANE // LANES) + n
+                out_ref[pl.ds(row, SUBLANES, stride=each_x), :] = value[
+                    x : x + SUBLANES, n * LANES : (n + 1) * LANES
+                ]
+    for x in range(0, BOX, SUBLANES):
+        for n in range(share * (PLANE // LANES), each_x):
+            out_ref[pl.ds(x * each_x + n, SUBLANES, stride=each_x), :] = note
 
 
 VMEM = pl.BlockSpec(memory_space=pltpu.VMEM)
@@ -340,38 +379,42 @@
     return lax.ppermute(array, "grp", pairs)
 
 
-def summed(target, weight, terms, held):
+def summed(target, terms, share, shape):
+    scratch = pltpu.VMEM(((shape[0] + 1) * shape[1] * PLANE // LANES, LANES), terms.dtype)
     return pl.pallas_call(
-        sum_kernel,
-        out_shape=jax.ShapeDtypeStruct((held, *terms.shape[1:]), terms.dtype),
-        in_specs=[SMEM, SMEM, VMEM],
+        functools.partial(sum_kernel, share, shape[1]),
+        out_shape=jax.ShapeDtypeStruct(shape, terms.dtype),
+        in_specs=[SMEM, VMEM],
         out_specs=VMEM,
-        scratch_shapes=[pltpu.VMEM((held, *terms.shape[1:]), terms.dtype)] * 3,
+        scratch_shapes=[scratch] * 4,
         compiler_params=ROWS_LIMIT,
         name="sum_rows",
-    )(target, weight, terms)
-
-
-def pair_terms(homes, boxes, local, moves, table, green, sine):
-    share = moves.shape[0] // 3
+    )(target, terms)
+
+
+def pair_terms(homes, share, boxes, local, moves, table, green, sine):
     cube = pltpu.VMEM((share * BOX, PLANE), jnp.float32)
+    depth = boxes.shape[1]
+    each_x = share * (PLANE // LANES) + SUBLANES // depth
     halves_type = pltpu.VMEM((4, HALF, HALF), jnp.bfloat16)
     return pl.pallas_call(
         functools.partial(solve_kernel, homes, share),
-        out_shape=jax.ShapeDtypeStruct(boxes.shape, jnp.float32),
-        in_specs=[SMEM, VMEM, VMEM, VMEM, HBM, HBM],
+        out_shape=jax.ShapeDtypeStruct((BOX * each_x, LANES), jnp.float32),
+        in_specs=[VMEM, VMEM, HBM, HBM, HBM, HBM],
         out_specs=VMEM,
         scratch_shapes=[
             cube,
             cube,
             cube,
+            pltpu.SMEM(moves.shape, jnp.int32),
+            pltpu.VMEM((BOX, BOX), jnp.float32),
             pltpu.VMEM((BOX, PLANE), jnp.float32),
             halves_type,
-            pltpu.SemaphoreType.DMA((5,)),
+            pltpu.SemaphoreType.DMA((7,)),
         ],
         compiler_params=SOLVE_LIMIT,
         name="pair_terms",
-    )(moves, boxes, local, sine, green, table)
+    )(boxes, local, moves, sine, green, table)
 
 
 def per_device(orbitals, pair_list, offsets):
@@ -439,10 +482,14 @@
     wanted = me * CAP + jnp.arange(CAP, dtype=jnp.int32)
     asked = slot_of[:, None, :] == wanted[None, :, None]
     home_second = jnp.sum(jnp.where(asked, second_of[:, None, :], 0), axis=2).reshape(slot_count)
-    local = jnp.concatenate(
-        [home_second.reshape(layers, slots_each), first_local.reshape(layers, rows_each)], axis=1
+    home_valid = jnp.any(asked, axis=2).reshape(slot_count)
+    target = jnp.concatenate(
+        [
+            jnp.where(home_valid, home_second, held).reshape(layers, slots_each),
+            first_local.reshape(layers, rows_each),
+        ],
+        axis=1,
     ).reshape(-1)
-    home_valid = jnp.any(asked, axis=2).reshape(slot_count)
     home_first = jnp.sum(jnp.where(asked, first_of[:, None, :], 0), axis=2).reshape(slot_count)
     from_rows = (slot // CAP * (2 * CAP) + slot % CAP).reshape(layers, rows_each)
     from_slots = (slot_ids // CAP * (2 * CAP) + CAP + slot_ids % CAP).reshape(layers, slots_each)
@@ -467,20 +514,14 @@
     signs = (first_ids[:, None] == ids).astype(jnp.int32) - (
         second_ids[:, None] == ids
     ).astype(jnp.int32)
-    moves = jnp.sum(signs[:, None, :] * offsets.T[None, :, :], axis=2).reshape(-1)
+    moves = jnp.sum(signs[:, None, :] * offsets.T[None, :, :], axis=2)
+    moves = jnp.pad(moves, ((0, -moves.shape[0] % 8), (0, LANES - moves.shape[1])))
     sine = sine_table()
     table = plane_tables(sine)
     green = green_rows()
-    weight = jnp.concatenate(
-        [
-            jnp.where(home_valid, 1.0, 0.0).reshape(layers, slots_each),
-            jnp.ones((layers, rows_each), jnp.float32),
-        ],
-        axis=1,
-    ).reshape(-1)
-    incoming, from_incoming, whole, moves, sine, table, green, local, weight = (
+    incoming, from_incoming, whole, moves, sine, table, green, target = (
         lax.optimization_barrier(
-            (incoming, from_incoming, whole, moves, sine, table, green, local, weight)
+            (incoming, from_incoming, whole, moves, sine, table, green, target)
         )
     )
 
@@ -494,9 +535,10 @@
         incoming,
     )
     boxes = swap(boxes, "grp")
-    terms = pair_terms(slots_each, boxes, whole, moves, table, green, sine)
-    terms = swap(terms, "grp")
-    return summed(local, weight, terms, held)
+    terms = pair_terms(slots_each, each, boxes, whole, moves, table, green, sine)
+    terms = terms.reshape(layers, -1, LANES).astype(jnp.float16)
+    terms = swap(terms, "grp").astype(jnp.float32)
+    return summed(target, terms, each, orbitals.shape)
 
 
 def solution(mesh):

time: 93 us -> 89.2 us (0.959)
  blocking collectives: 31.4 us -> 27.7 us
    all_to_all x1, blocking collectives: 15.5 us -> 11.8 us  [per_device(): terms = swap(terms, 'grp').astype(jnp.float32)]
  transfers between devices with their start and end apart: 7 -> 7, of which waited for: 1 -> 1; matrix products, arithmetic and copies ran while one was open for 5% -> 5% of each run, Pallas kernels for 3% -> 4%
where the time goes in v5:
time: 89.2 us; the launch traced here: 88.5 us
  starting transfers between devices  38 us (43%)
  blocking collectives  27.7 us (31%)
  Pallas kernels  13.5 us (15%)
  waiting for transfers between devices  3.65 us (4%)
  local copies, waits for them, and re-layouts  2.95 us (3%)
  other arithmetic  2.42 us (3%)
    ppermute x6, starting transfers between devices, along(): return lax.ppermute(array, 'grp', pairs)  21.2 us
    all_to_all x1, starting transfers between devices, per_device(): incoming = swap(outgoing, 'orb')  16.7 us
    all_to_all x1, blocking collectives, per_device(): boxes = swap(boxes, 'grp')  16 us
    all_to_all x1, blocking collectives, per_device(): terms = swap(terms, 'grp').astype(jnp.float32)  11.8 us
    pallas_call x4, Pallas kernels, rows_call(): pl.pallas_call(kernel, out_shape=out, in_specs=in_specs, out_specs=(VMEM,...  4.84 us
    pallas_call x1, Pallas kernels, pair_terms(): pl.pallas_call(functools.partial(solve_kernel, homes, share), out_shape=j...  4.54 us
    all_to_all x1, waiting for transfers between devices, per_device(): incoming = swap(outgoing, 'orb')  3.63 us
    pallas_call x1, Pallas kernels, summed(): pl.pallas_call(functools.partial(sum_kernel, share, shape[1]), out_shape=...  2.06 us
  transfers between devices with their start and end apart: 7, of which 1 were waited for; matrix products, arithmetic and copies ran while one was open for 5% of the time, Pallas kernels for 4%

profile of v5, /device:TPU:1, one launch (start us, length us, event | category | flops | bytes accessed | tf_op | source)
XLA Modules:
  0.0 88.5 jit_solution(1184267109780046642)
XLA Ops:
  0.0 3.1 %pick_rows.1 = (bf16[128,2,1024]{2,1,0:T(2,128)(2,1)}, bf16[24,2,1024]{2,1,0:T(2,128)(2,1)}, bf16[24,2,1024]{2,1,0:T(2,128)(2,1)}, bf16[24,2,1024]{2,1,0:T(2,128)(2,1)}, bf16[24,2,1024]{2,1,0:T(2,128)(2,1)}) custom-call(s32[3,32,32]{2,1,0:T(8,128)} %bitcast.12, bf16[64,2,1024]{2,1,0:T(2,128)(2,1)} %orbitals_ref.1), custom_call_target="tpu_custom_call" | custom-call | tf_op jit(solution)/shard_map/pick_rows/pallas_call | solution.py:362
  3.1 16.7 %all-to-all-start = ((bf16[128,2,1024]{2,1,0:T(2,128)(2,1)}), bf16[128,2,1024]{2,1,0:T(2,128)(2,1)S(1)}, u32[]{:S(2)}, u32[]{:S(2)}) async-start(bf16[128,2,1024]{2,1,0:T(2,128)(2,1)} %get-tuple-element.25), calls=%async_computation | async-start | bytes 1048576 | tf_op jit(solution)/shard_map/all_to_all | solution.py:452
  19.8 3.1 %collective-permute-start = (bf16[24,2,1024]{2,1,0:T(2,128)(2,1)}, bf16[24,2,1024]{2,1,0:T(2,128)(2,1)S(1)}, u32[]{:S(2)}, u32[]{:S(2)}) collective-permute-start(bf16[24,2,1024]{2,1,0:T(2,128)(2,1)} %get-tuple-element.28), channel_id=1, source_target_pairs={{0,1},{1,2},{2,3},{3,0},{4,5},{5,6},{6,7},{7,4},{8,9},{9,10},{10,1... | collective-permute-start | bytes 294920 | tf_op jit(solution)/shard_map/ppermute | solution.py:379
  23.0 4.4 %collective-permute-start.1 = (bf16[24,2,1024]{2,1,0:T(2,128)(2,1)}, bf16[24,2,1024]{2,1,0:T(2,128)(2,1)S(1)}, u32[]{:S(2)}, u32[]{:S(2)}) collective-permute-start(bf16[24,2,1024]{2,1,0:T(2,128)(2,1)} %get-tuple-element.29), channel_id=1, source_target_pairs={{0,2},{1,3},{2,0},{3,1},{4,6},{5,7},{6,4},{7,5},{8,10},{9,11},{10,... | collective-permute-start | bytes 294920 | tf_op jit(solution)/shard_map/ppermute | solution.py:379
  27.3 3.1 %collective-permute-start.2 = (bf16[24,2,1024]{2,1,0:T(2,128)(2,1)}, bf16[24,2,1024]{2,1,0:T(2,128)(2,1)S(1)}, u32[]{:S(2)}, u32[]{:S(2)}) collective-permute-start(bf16[24,2,1024]{2,1,0:T(2,128)(2,1)} %get-tuple-element.30), channel_id=1, source_target_pairs={{0,3},{1,0},{2,1},{3,2},{4,7},{5,4},{6,5},{7,6},{8,11},{9,8},{10,9... | collective-permute-start | bytes 294920 | tf_op jit(solution)/shard_map/ppermute | solution.py:379
  30.4 0.8 slice_bitcast_fusion
  31.2 0.2 compare_reduce_fusion
  31.4 0.2 fusion
  31.6 0.1 select_reduce_fusion.1
  31.7 0.1 reduce_sum.57
  31.9 0.1 pad_add_fusion
  31.9 0.1 reshape.129
  32.0 0.1 dynamic_slice.15
  32.1 0.1 dynamic_slice.13
  32.2 0.1 reshape.127.picks_ref
  32.3 0.1 copy.7
  32.4 0.1 select_n.92
  32.4 0.1 pad_add_fusion.1
  32.5 0.1 reshape.130.target_ref
  32.6 0.1 copy.4
  32.7 0.1 reshape.128
  32.8 0.1 copy.5
  32.9 0.1 add.173
  33.0 0.1 dynamic_slice.12
  33.1 0.1 dynamic_slice.14
  33.2 0.1 pad_add_fusion.3
  33.3 0.1 pad_add_fusion.4
  33.4 0.1 fusion.25
  33.4 0.1 sine_multiply_fusion.sine_ref.sine_hbm
  33.6 0.1 add_divide_fusion.green_hbm
  33.7 0.1 convert_subtract_fusion
  33.8 0.1 pad_add_fusion.2.place_ref
  33.8 0.0 collective-permute-done.refs_1_
  33.8 0.0 collective-permute-done.1.refs_2_
  33.9 0.0 collective-permute-done.2.refs_3_
  33.9 0.0 copy-start
  33.9 0.9 copy-done
  34.8 0.6 turn_rows.1
  35.3 3.2 %collective-permute-start.3 = (bf16[24,2,1024]{2,1,0:T(2,128)(2,1)S(1)}, bf16[24,2,1024]{2,1,0:T(2,128)(2,1)S(1)}, u32[]{:S(2)}, u32[]{:S(2)}) collective-permute-start(bf16[24,2,1024]{2,1,0:T(2,128)(2,1)S(1)} %get-tuple-element.32), channel_id=1, source_target_pairs={{0,4},{1,5},{2,6},{3,7},{4,8},{5,9},{6,10},{7,11},{8,12},{9,13},{1... | collective-permute-start | bytes 294920 | tf_op jit(solution)/shard_map/ppermute | solution.py:379
  38.5 4.5 %collective-permute-start.4 = (bf16[24,2,1024]{2,1,0:T(2,128)(2,1)S(1)}, bf16[24,2,1024]{2,1,0:T(2,128)(2,1)S(1)}, u32[]{:S(2)}, u32[]{:S(2)}) collective-permute-start(bf16[24,2,1024]{2,1,0:T(2,128)(2,1)S(1)} %get-tuple-element.33), channel_id=1, source_target_pairs={{0,8},{1,9},{2,10},{3,11},{4,12},{5,13},{6,14},{7,15},{8,0},{9,1},... | collective-permute-start | bytes 294920 | tf_op jit(solution)/shard_map/ppermute | solution.py:379
  43.1 3.0 %collective-permute-start.5 = (bf16[24,2,1024]{2,1,0:T(2,128)(2,1)S(1)}, bf16[24,2,1024]{2,1,0:T(2,128)(2,1)S(1)}, u32[]{:S(2)}, u32[]{:S(2)}) collective-permute-start(bf16[24,2,1024]{2,1,0:T(2,128)(2,1)S(1)} %get-tuple-element.34), channel_id=1, source_target_pairs={{0,12},{1,13},{2,14},{3,15},{4,0},{5,1},{6,2},{7,3},{8,4},{9,5},{1... | collective-permute-start | bytes 294920 | tf_op jit(solution)/shard_map/ppermute | solution.py:379
  46.1 0.9 %multiply_reduce_fusion = s32[6,3]{0,1:T(4,128)S(1)} fusion(s32[3,2048]{1,0:T(4,128)} %bitcast.14, s32[6,2048]{1,0:T(8,128)S(1)} %convert_subtract_fusion), kind=kLoop, calls=%fused_computation | loop fusion | flops 73710 | bytes 73800 | tf_op jit(solution)/shard_map/reduce_sum | solution.py:517
  47.0 0.1 copy.6
  47.1 2.0 %plane_tables.1.table_hbm = bf16[40,512,512]{2,1,0:T(8,128)(2,1)} custom-call(f32[32,32]{1,0:T(8,128)S(1)} %sine_multiply_fusion.sine_ref.sine_hbm), custom_call_target="tpu_custom_call" | custom-call | tf_op jit(solution)/shard_map/plane_tables/pallas_call | solution.py:91
  49.1 0.0 collective-permute-done.3.refs_1_
  49.1 0.0 collective-permute-done.4.refs_2_
  49.1 0.0 collective-permute-done.5.refs_3_
  49.1 0.6 settle_rows.1.local_ref
  49.7 3.6 %all-to-all-done.incoming_ref = bf16[128,2,1024]{2,1,0:T(2,128)(2,1)S(1)} async-done(((bf16[128,2,1024]{2,1,0:T(2,128)(2,1)}), bf16[128,2,1024]{2,1,0:T(2,128)(2,1)S(1)}, u32[]{:S(2)}, u32[]{:S(2)}) %all-to-all-start) | async-done | bytes 524320 | tf_op jit(solution)/shard_map/all_to_all | solution.py:452
  53.4 0.6 pack_rows.1
  54.0 16.0 %all_to_all.15.boxes_ref = bf16[96,2,1024]{2,1,0:T(2,128)(2,1)S(1)} all-to-all(bf16[96,2,1024]{2,1,0:T(2,128)(2,1)S(1)} %pack_rows.1), channel_id=1, replica_groups=mesh['orb'=32,'grp'=16] {'grp'}, dimensions={0} | all-to-all | bytes 786432 | tf_op jit(solution)/shard_map/all_to_all | solution.py:537
  69.9 4.5 %pair_terms.1 = f32[1664,128]{1,0:T(8,128)S(1)} custom-call(bf16[96,2,1024]{2,1,0:T(2,128)(2,1)S(1)} %all_to_all.15.boxes_ref, bf16[96,2,1024]{2,1,0:T(2,128)(2,1)S(1)} %settle_rows.1.local_ref, s32[8,128]{1,0:T(8,128)S(1)} %pad.4.moves_hbm, f32[32,32]{1,0:T(8,128)S(1)} %sine_multiply_fusion.sine_ref.sine_hbm, f32[32,1024]{1,0:T(8,128)S(1)} %add_divide_fusion.green_hbm, ...), custom_call_target="tpu_custom_call" | custom-call | tf_op jit(solution)/shard_map/pair_terms/pallas_call | solution.py:400
  74.5 0.1 convert_element_type.61
  74.6 11.8 %all_to_all.16 = f16[16,104,128]{2,1,0:T(8,128)(2,1)S(1)} all-to-all(f16[16,104,128]{2,1,0:T(8,128)(2,1)S(1)} %bitcast.11), channel_id=1, replica_groups=mesh['orb'=32,'grp'=16] {'grp'}, dimensions={0} | all-to-all | bytes 851968 | tf_op jit(solution)/shard_map/all_to_all | solution.py:540
  86.3 0.1 convert_element_type.63.terms_ref
  86.4 2.1 %sum_rows.1 = f32[64,2,1024]{2,1,0:T(2,128)} custom-call(s32[96]{0:T(128)S(1)} %reshape.130.target_ref, f32[16,104,128]{2,1,0:T(8,128)S(1)} %convert_element_type.63.terms_ref), custom_call_target="tpu_custom_call" | custom-call | tf_op jit(solution)/shard_map/sum_rows/pallas_call | solution.py:384
  (10 shorter events, 0.1 us)
Async XLA Ops:
  3.1 50.3 %all-to-all-start = ((bf16[128,2,1024]{2,1,0:T(2,128)(2,1)}), bf16[128,2,1024]{2,1,0:T(2,128)(2,1)S(1)}, u32[]{:S(2)}, u32[]{:S(2)}) async-start(bf16[128,2,1024]{2,1,0:T(2,128)(2,1)} %get-tuple-element.25), calls=%async_computation | async-start | bytes 1048576 | tf_op jit(solution)/shard_map/all_to_all | solution.py:452
  19.8 14.0 %collective-permute-start = (bf16[24,2,1024]{2,1,0:T(2,128)(2,1)}, bf16[24,2,1024]{2,1,0:T(2,128)(2,1)S(1)}, u32[]{:S(2)}, u32[]{:S(2)}) collective-permute-start(bf16[24,2,1024]{2,1,0:T(2,128)(2,1)} %get-tuple-element.28), channel_id=1, source_target_pairs={{0,1},{1,2},{2,3},{3,0},{4,5},{5,6},{6,7},{7,4},{8,9},{9,10},{10,1... | collective-permute-start | bytes 294920 | tf_op jit(solution)/shard_map/ppermute | solution.py:379
  23.0 10.9 %collective-permute-start.1 = (bf16[24,2,1024]{2,1,0:T(2,128)(2,1)}, bf16[24,2,1024]{2,1,0:T(2,128)(2,1)S(1)}, u32[]{:S(2)}, u32[]{:S(2)}) collective-permute-start(bf16[24,2,1024]{2,1,0:T(2,128)(2,1)} %get-tuple-element.29), channel_id=1, source_target_pairs={{0,2},{1,3},{2,0},{3,1},{4,6},{5,7},{6,4},{7,5},{8,10},{9,11},{10,... | collective-permute-start | bytes 294920 | tf_op jit(solution)/shard_map/ppermute | solution.py:379
  27.3 6.5 %collective-permute-start.2 = (bf16[24,2,1024]{2,1,0:T(2,128)(2,1)}, bf16[24,2,1024]{2,1,0:T(2,128)(2,1)S(1)}, u32[]{:S(2)}, u32[]{:S(2)}) collective-permute-start(bf16[24,2,1024]{2,1,0:T(2,128)(2,1)} %get-tuple-element.30), channel_id=1, source_target_pairs={{0,3},{1,0},{2,1},{3,2},{4,7},{5,4},{6,5},{7,6},{8,11},{9,8},{10,9... | collective-permute-start | bytes 294920 | tf_op jit(solution)/shard_map/ppermute | solution.py:379
  33.9 0.9 %copy-start = (bf16[24,2,1024]{2,1,0:T(2,128)(2,1)S(1)}, bf16[24,2,1024]{2,1,0:T(2,128)(2,1)}, u32[]{:S(2)}) copy-start(bf16[24,2,1024]{2,1,0:T(2,128)(2,1)} %get-tuple-element.27.refs_0_) | copy-start | bytes 294916
  35.3 13.8 %collective-permute-start.3 = (bf16[24,2,1024]{2,1,0:T(2,128)(2,1)S(1)}, bf16[24,2,1024]{2,1,0:T(2,128)(2,1)S(1)}, u32[]{:S(2)}, u32[]{:S(2)}) collective-permute-start(bf16[24,2,1024]{2,1,0:T(2,128)(2,1)S(1)} %get-tuple-element.32), channel_id=1, source_target_pairs={{0,4},{1,5},{2,6},{3,7},{4,8},{5,9},{6,10},{7,11},{8,12},{9,13},{1... | collective-permute-start | bytes 294920 | tf_op jit(solution)/shard_map/ppermute | solution.py:379
  38.5 10.6 %collective-permute-start.4 = (bf16[24,2,1024]{2,1,0:T(2,128)(2,1)S(1)}, bf16[24,2,1024]{2,1,0:T(2,128)(2,1)S(1)}, u32[]{:S(2)}, u32[]{:S(2)}) collective-permute-start(bf16[24,2,1024]{2,1,0:T(2,128)(2,1)S(1)} %get-tuple-element.33), channel_id=1, source_target_pairs={{0,8},{1,9},{2,10},{3,11},{4,12},{5,13},{6,14},{7,15},{8,0},{9,1},... | collective-permute-start | bytes 294920 | tf_op jit(solution)/shard_map/ppermute | solution.py:379
  43.1 6.1 %collective-permute-start.5 = (bf16[24,2,1024]{2,1,0:T(2,128)(2,1)S(1)}, bf16[24,2,1024]{2,1,0:T(2,128)(2,1)S(1)}, u32[]{:S(2)}, u32[]{:S(2)}) collective-permute-start(bf16[24,2,1024]{2,1,0:T(2,128)(2,1)S(1)} %get-tuple-element.34), channel_id=1, source_target_pairs={{0,12},{1,13},{2,14},{3,15},{4,0},{5,1},{6,2},{7,3},{8,4},{9,5},{1... | collective-permute-start | bytes 294920 | tf_op jit(solution)/shard_map/ppermute | solution.py:379

commit v6 on v5

--- a/solution.py
+++ b/solution.py
@@ -190,12 +190,10 @@
                 for x in range(depth)
             ]
             held[at, :] = held[at, :] + jnp.concatenate(term, 0) * gains[:, k : k + 1]
-    total = sums[0]
-    total[...] = sum(held[...] for held in sums)
-    for n in range(out_ref.shape[0]):
-        for c in range(chunks):
-            cells = pl.ds(n * block + c, depth, stride=chunks)
-            out_ref[n, :, c * LANES : (c + 1) * LANES] = total[cells, :]
+    for n in range(out_ref.shape[0] // chunks):
+        part = slice(n * chunks, (n + 1) * chunks)
+        first_row = n // depth * block + n % depth
+        out_ref[pl.ds(first_row, chunks, stride=depth), :] = sum(held[part, :] for held in sums)
 
 
 def same_pair():
@@ -383,7 +381,7 @@
     scratch = pltpu.VMEM(((shape[0] + 1) * shape[1] * PLANE // LANES, LANES), terms.dtype)
     return pl.pallas_call(
         functools.partial(sum_kernel, share, shape[1]),
-        out_shape=jax.ShapeDtypeStruct(shape, terms.dtype),
+        out_shape=jax.ShapeDtypeStruct((math.prod(shape) // LANES, LANES), terms.dtype),
         in_specs=[SMEM, VMEM],
         out_specs=VMEM,
         scratch_shapes=[scratch] * 4,
@@ -538,7 +536,9 @@
     terms = pair_terms(slots_each, each, boxes, whole, moves, table, green, sine)
     terms = terms.reshape(layers, -1, LANES).astype(jnp.float16)
     terms = swap(terms, "grp").astype(jnp.float32)
-    return summed(target, terms, each, orbitals.shape)
+    action = summed(target, terms, each, orbitals.shape)
+    action = action.reshape(held, plane // LANES, depth, LANES)
+    return jnp.swapaxes(action, 1, 2).reshape(orbitals.shape)
 
 
 def solution(mesh):

time: 89.2 us -> 88.9 us (level)
  no operation moved by 1% of the time
where the time goes in v6:
time: 88.9 us; the launch traced here: 88.1 us
  starting transfers between devices  38 us (43%)
  blocking collectives  27.7 us (31%)
  Pallas kernels  13.2 us (15%)
  waiting for transfers between devices  3.65 us (4%)
  local copies, waits for them, and re-layouts  2.95 us (3%)
  other arithmetic  2.42 us (3%)
    ppermute x6, starting transfers between devices, along(): return lax.ppermute(array, 'grp', pairs)  21.2 us
    all_to_all x1, starting transfers between devices, per_device(): incoming = swap(outgoing, 'orb')  16.7 us
    all_to_all x1, blocking collectives, per_device(): boxes = swap(boxes, 'grp')  16 us
    all_to_all x1, blocking collectives, per_device(): terms = swap(terms, 'grp').astype(jnp.float32)  11.8 us
    pallas_call x4, Pallas kernels, rows_call(): pl.pallas_call(kernel, out_shape=out, in_specs=in_specs, out_specs=(VMEM,...  4.84 us
    pallas_call x1, Pallas kernels, pair_terms(): pl.pallas_call(functools.partial(solve_kernel, homes, share), out_shape=j...  4.54 us
    all_to_all x1, waiting for transfers between devices, per_device(): incoming = swap(outgoing, 'orb')  3.63 us
    pallas_call x1, Pallas kernels, plane_tables(): pl.pallas_call(plane_kernel, out_shape=jax.ShapeDtypeStruct((TABLES, HALF...  2.02 us
  transfers between devices with their start and end apart: 7, of which 1 were waited for; matrix products, arithmetic and copies ran while one was open for 5% of the time, Pallas kernels for 4%

profile of v6, /device:TPU:1, one launch (start us, length us, event | category | flops | bytes accessed | tf_op | source)
XLA Modules:
  0.0 88.1 jit_solution(2258957902209712858)
XLA Ops:
  0.0 3.1 %pick_rows.1 = (bf16[128,2,1024]{2,1,0:T(2,128)(2,1)}, bf16[24,2,1024]{2,1,0:T(2,128)(2,1)}, bf16[24,2,1024]{2,1,0:T(2,128)(2,1)}, bf16[24,2,1024]{2,1,0:T(2,128)(2,1)}, bf16[24,2,1024]{2,1,0:T(2,128)(2,1)}) custom-call(s32[3,32,32]{2,1,0:T(8,128)} %bitcast.17, bf16[64,2,1024]{2,1,0:T(2,128)(2,1)} %orbitals_ref.1), custom_call_target="tpu_custom_call" | custom-call | tf_op jit(solution)/shard_map/pick_rows/pallas_call | solution.py:360
  3.1 16.7 %all-to-all-start = ((bf16[128,2,1024]{2,1,0:T(2,128)(2,1)}), bf16[128,2,1024]{2,1,0:T(2,128)(2,1)S(1)}, u32[]{:S(2)}, u32[]{:S(2)}) async-start(bf16[128,2,1024]{2,1,0:T(2,128)(2,1)} %get-tuple-element.25), calls=%async_computation | async-start | bytes 1048576 | tf_op jit(solution)/shard_map/all_to_all | solution.py:450
  19.8 3.1 %collective-permute-start = (bf16[24,2,1024]{2,1,0:T(2,128)(2,1)}, bf16[24,2,1024]{2,1,0:T(2,128)(2,1)S(1)}, u32[]{:S(2)}, u32[]{:S(2)}) collective-permute-start(bf16[24,2,1024]{2,1,0:T(2,128)(2,1)} %get-tuple-element.28), channel_id=1, source_target_pairs={{0,1},{1,2},{2,3},{3,0},{4,5},{5,6},{6,7},{7,4},{8,9},{9,10},{10,1... | collective-permute-start | bytes 294920 | tf_op jit(solution)/shard_map/ppermute | solution.py:377
  23.0 4.4 %collective-permute-start.1 = (bf16[24,2,1024]{2,1,0:T(2,128)(2,1)}, bf16[24,2,1024]{2,1,0:T(2,128)(2,1)S(1)}, u32[]{:S(2)}, u32[]{:S(2)}) collective-permute-start(bf16[24,2,1024]{2,1,0:T(2,128)(2,1)} %get-tuple-element.29), channel_id=1, source_target_pairs={{0,2},{1,3},{2,0},{3,1},{4,6},{5,7},{6,4},{7,5},{8,10},{9,11},{10,... | collective-permute-start | bytes 294920 | tf_op jit(solution)/shard_map/ppermute | solution.py:377
  27.3 3.1 %collective-permute-start.2 = (bf16[24,2,1024]{2,1,0:T(2,128)(2,1)}, bf16[24,2,1024]{2,1,0:T(2,128)(2,1)S(1)}, u32[]{:S(2)}, u32[]{:S(2)}) collective-permute-start(bf16[24,2,1024]{2,1,0:T(2,128)(2,1)} %get-tuple-element.30), channel_id=1, source_target_pairs={{0,3},{1,0},{2,1},{3,2},{4,7},{5,4},{6,5},{7,6},{8,11},{9,8},{10,9... | collective-permute-start | bytes 294920 | tf_op jit(solution)/shard_map/ppermute | solution.py:377
  30.4 0.8 slice_bitcast_fusion
  31.2 0.2 compare_reduce_fusion
  31.4 0.2 fusion
  31.6 0.1 select_reduce_fusion.1
  31.7 0.1 reduce_sum.57
  31.9 0.1 pad_add_fusion
  31.9 0.1 reshape.135
  32.0 0.1 dynamic_slice.15
  32.1 0.1 dynamic_slice.13
  32.2 0.1 reshape.133.picks_ref
  32.3 0.1 copy.9
  32.4 0.1 select_n.92
  32.4 0.1 pad_add_fusion.1
  32.5 0.1 reshape.136.target_ref
  32.6 0.1 copy.6
  32.7 0.1 reshape.134
  32.8 0.1 copy.7
  32.9 0.1 add.173
  33.0 0.1 dynamic_slice.12
  33.1 0.1 dynamic_slice.14
  33.2 0.1 pad_add_fusion.3
  33.3 0.1 pad_add_fusion.4
  33.4 0.1 fusion.25
  33.4 0.1 sine_multiply_fusion.sine_ref.sine_hbm
  33.6 0.1 add_divide_fusion.green_hbm
  33.7 0.1 convert_subtract_fusion
  33.8 0.1 pad_add_fusion.2.place_ref
  33.8 0.0 collective-permute-done.refs_1_
  33.8 0.0 collective-permute-done.1.refs_2_
  33.9 0.0 collective-permute-done.2.refs_3_
  33.9 0.0 copy-start
  33.9 0.9 %copy-done = bf16[24,2,1024]{2,1,0:T(2,128)(2,1)S(1)} copy-done((bf16[24,2,1024]{2,1,0:T(2,128)(2,1)S(1)}, bf16[24,2,1024]{2,1,0:T(2,128)(2,1)}, u32[]{:S(2)}) %copy-start) | copy-done | bytes 98328
  34.8 0.6 turn_rows.1
  35.3 3.2 %collective-permute-start.3 = (bf16[24,2,1024]{2,1,0:T(2,128)(2,1)S(1)}, bf16[24,2,1024]{2,1,0:T(2,128)(2,1)S(1)}, u32[]{:S(2)}, u32[]{:S(2)}) collective-permute-start(bf16[24,2,1024]{2,1,0:T(2,128)(2,1)S(1)} %get-tuple-element.32), channel_id=1, source_target_pairs={{0,4},{1,5},{2,6},{3,7},{4,8},{5,9},{6,10},{7,11},{8,12},{9,13},{1... | collective-permute-start | bytes 294920 | tf_op jit(solution)/shard_map/ppermute | solution.py:377
  38.5 4.5 %collective-permute-start.4 = (bf16[24,2,1024]{2,1,0:T(2,128)(2,1)S(1)}, bf16[24,2,1024]{2,1,0:T(2,128)(2,1)S(1)}, u32[]{:S(2)}, u32[]{:S(2)}) collective-permute-start(bf16[24,2,1024]{2,1,0:T(2,128)(2,1)S(1)} %get-tuple-element.33), channel_id=1, source_target_pairs={{0,8},{1,9},{2,10},{3,11},{4,12},{5,13},{6,14},{7,15},{8,0},{9,1},... | collective-permute-start | bytes 294920 | tf_op jit(solution)/shard_map/ppermute | solution.py:377
  43.1 3.0 %collective-permute-start.5 = (bf16[24,2,1024]{2,1,0:T(2,128)(2,1)S(1)}, bf16[24,2,1024]{2,1,0:T(2,128)(2,1)S(1)}, u32[]{:S(2)}, u32[]{:S(2)}) collective-permute-start(bf16[24,2,1024]{2,1,0:T(2,128)(2,1)S(1)} %get-tuple-element.34), channel_id=1, source_target_pairs={{0,12},{1,13},{2,14},{3,15},{4,0},{5,1},{6,2},{7,3},{8,4},{9,5},{1... | collective-permute-start | bytes 294920 | tf_op jit(solution)/shard_map/ppermute | solution.py:377
  46.1 0.9 %multiply_reduce_fusion = s32[6,3]{0,1:T(4,128)S(1)} fusion(s32[3,2048]{1,0:T(4,128)} %bitcast.19, s32[6,2048]{1,0:T(8,128)S(1)} %convert_subtract_fusion), kind=kLoop, calls=%fused_computation | loop fusion | flops 73710 | bytes 73800 | tf_op jit(solution)/shard_map/reduce_sum | solution.py:515
  47.0 0.1 copy.8
  47.1 2.0 %plane_tables.1.table_hbm = bf16[40,512,512]{2,1,0:T(8,128)(2,1)} custom-call(f32[32,32]{1,0:T(8,128)S(1)} %sine_multiply_fusion.sine_ref.sine_hbm), custom_call_target="tpu_custom_call" | custom-call | tf_op jit(solution)/shard_map/plane_tables/pallas_call | solution.py:91
  49.1 0.0 collective-permute-done.3.refs_1_
  49.1 0.0 collective-permute-done.4.refs_2_
  49.1 0.0 collective-permute-done.5.refs_3_
  49.1 0.6 settle_rows.1.local_ref
  49.7 3.6 %all-to-all-done.incoming_ref = bf16[128,2,1024]{2,1,0:T(2,128)(2,1)S(1)} async-done(((bf16[128,2,1024]{2,1,0:T(2,128)(2,1)}), bf16[128,2,1024]{2,1,0:T(2,128)(2,1)S(1)}, u32[]{:S(2)}, u32[]{:S(2)}) %all-to-all-start) | async-done | bytes 524320 | tf_op jit(solution)/shard_map/all_to_all | solution.py:450
  53.4 0.6 pack_rows.1
  54.0 16.0 %all_to_all.15.boxes_ref = bf16[96,2,1024]{2,1,0:T(2,128)(2,1)S(1)} all-to-all(bf16[96,2,1024]{2,1,0:T(2,128)(2,1)S(1)} %pack_rows.1), channel_id=1, replica_groups=mesh['orb'=32,'grp'=16] {'grp'}, dimensions={0} | all-to-all | bytes 786432 | tf_op jit(solution)/shard_map/all_to_all | solution.py:535
  69.9 4.5 %pair_terms.1 = f32[1664,128]{1,0:T(8,128)S(1)} custom-call(bf16[96,2,1024]{2,1,0:T(2,128)(2,1)S(1)} %all_to_all.15.boxes_ref, bf16[96,2,1024]{2,1,0:T(2,128)(2,1)S(1)} %settle_rows.1.local_ref, s32[8,128]{1,0:T(8,128)S(1)} %pad.4.moves_hbm, f32[32,32]{1,0:T(8,128)S(1)} %sine_multiply_fusion.sine_ref.sine_hbm, f32[32,1024]{1,0:T(8,128)S(1)} %add_divide_fusion.green_hbm, ...), custom_call_target="tpu_custom_call" | custom-call | tf_op jit(solution)/shard_map/pair_terms/pallas_call | solution.py:398
  74.5 0.1 convert_element_type.61
  74.6 11.8 %all_to_all.16 = f16[16,104,128]{2,1,0:T(8,128)(2,1)S(1)} all-to-all(f16[16,104,128]{2,1,0:T(8,128)(2,1)S(1)} %bitcast.16), channel_id=1, replica_groups=mesh['orb'=32,'grp'=16] {'grp'}, dimensions={0} | all-to-all | bytes 851968 | tf_op jit(solution)/shard_map/all_to_all | solution.py:538
  86.3 0.1 convert_element_type.63.terms_ref
  86.4 1.8 %sum_rows.1 = f32[1024,128]{1,0:T(8,128)} custom-call(s32[96]{0:T(128)S(1)} %reshape.136.target_ref, f32[16,104,128]{2,1,0:T(8,128)S(1)} %convert_element_type.63.terms_ref), custom_call_target="tpu_custom_call" | custom-call | tf_op jit(solution)/shard_map/sum_rows/pallas_call | solution.py:382
  (10 shorter events, 0.1 us)
Async XLA Ops:
  3.1 50.3 %all-to-all-start = ((bf16[128,2,1024]{2,1,0:T(2,128)(2,1)}), bf16[128,2,1024]{2,1,0:T(2,128)(2,1)S(1)}, u32[]{:S(2)}, u32[]{:S(2)}) async-start(bf16[128,2,1024]{2,1,0:T(2,128)(2,1)} %get-tuple-element.25), calls=%async_computation | async-start | bytes 1048576 | tf_op jit(solution)/shard_map/all_to_all | solution.py:450
  19.8 14.0 %collective-permute-start = (bf16[24,2,1024]{2,1,0:T(2,128)(2,1)}, bf16[24,2,1024]{2,1,0:T(2,128)(2,1)S(1)}, u32[]{:S(2)}, u32[]{:S(2)}) collective-permute-start(bf16[24,2,1024]{2,1,0:T(2,128)(2,1)} %get-tuple-element.28), channel_id=1, source_target_pairs={{0,1},{1,2},{2,3},{3,0},{4,5},{5,6},{6,7},{7,4},{8,9},{9,10},{10,1... | collective-permute-start | bytes 294920 | tf_op jit(solution)/shard_map/ppermute | solution.py:377
  23.0 10.9 %collective-permute-start.1 = (bf16[24,2,1024]{2,1,0:T(2,128)(2,1)}, bf16[24,2,1024]{2,1,0:T(2,128)(2,1)S(1)}, u32[]{:S(2)}, u32[]{:S(2)}) collective-permute-start(bf16[24,2,1024]{2,1,0:T(2,128)(2,1)} %get-tuple-element.29), channel_id=1, source_target_pairs={{0,2},{1,3},{2,0},{3,1},{4,6},{5,7},{6,4},{7,5},{8,10},{9,11},{10,... | collective-permute-start | bytes 294920 | tf_op jit(solution)/shard_map/ppermute | solution.py:377
  27.3 6.5 %collective-permute-start.2 = (bf16[24,2,1024]{2,1,0:T(2,128)(2,1)}, bf16[24,2,1024]{2,1,0:T(2,128)(2,1)S(1)}, u32[]{:S(2)}, u32[]{:S(2)}) collective-permute-start(bf16[24,2,1024]{2,1,0:T(2,128)(2,1)} %get-tuple-element.30), channel_id=1, source_target_pairs={{0,3},{1,0},{2,1},{3,2},{4,7},{5,4},{6,5},{7,6},{8,11},{9,8},{10,9... | collective-permute-start | bytes 294920 | tf_op jit(solution)/shard_map/ppermute | solution.py:377
  33.9 0.9 %copy-start = (bf16[24,2,1024]{2,1,0:T(2,128)(2,1)S(1)}, bf16[24,2,1024]{2,1,0:T(2,128)(2,1)}, u32[]{:S(2)}) copy-start(bf16[24,2,1024]{2,1,0:T(2,128)(2,1)} %get-tuple-element.27.refs_0_) | copy-start | bytes 294916
  35.3 13.8 %collective-permute-start.3 = (bf16[24,2,1024]{2,1,0:T(2,128)(2,1)S(1)}, bf16[24,2,1024]{2,1,0:T(2,128)(2,1)S(1)}, u32[]{:S(2)}, u32[]{:S(2)}) collective-permute-start(bf16[24,2,1024]{2,1,0:T(2,128)(2,1)S(1)} %get-tuple-element.32), channel_id=1, source_target_pairs={{0,4},{1,5},{2,6},{3,7},{4,8},{5,9},{6,10},{7,11},{8,12},{9,13},{1... | collective-permute-start | bytes 294920 | tf_op jit(solution)/shard_map/ppermute | solution.py:377
  38.5 10.6 %collective-permute-start.4 = (bf16[24,2,1024]{2,1,0:T(2,128)(2,1)S(1)}, bf16[24,2,1024]{2,1,0:T(2,128)(2,1)S(1)}, u32[]{:S(2)}, u32[]{:S(2)}) collective-permute-start(bf16[24,2,1024]{2,1,0:T(2,128)(2,1)S(1)} %get-tuple-element.33), channel_id=1, source_target_pairs={{0,8},{1,9},{2,10},{3,11},{4,12},{5,13},{6,14},{7,15},{8,0},{9,1},... | collective-permute-start | bytes 294920 | tf_op jit(solution)/shard_map/ppermute | solution.py:377
  43.1 6.1 %collective-permute-start.5 = (bf16[24,2,1024]{2,1,0:T(2,128)(2,1)S(1)}, bf16[24,2,1024]{2,1,0:T(2,128)(2,1)S(1)}, u32[]{:S(2)}, u32[]{:S(2)}) collective-permute-start(bf16[24,2,1024]{2,1,0:T(2,128)(2,1)S(1)} %get-tuple-element.34), channel_id=1, source_target_pairs={{0,12},{1,13},{2,14},{3,15},{4,0},{5,1},{6,2},{7,3},{8,4},{9,5},{1... | collective-permute-start | bytes 294920 | tf_op jit(solution)/shard_map/ppermute | solution.py:377
